TPU v7x, 64 devices: a 2x2x8 block of a 4x4x8 slice. The times are simulated.
64 devices in a mesh: dp: 4 (over x, y), sp: 16 (over z, core).
Axes of the slice: x: 2, y: 2, z: 8, core: 2. Of those that a mesh axis runs over, the one named last changes fastest.
The devices are a block of a 4x4x8 slice.
Arguments:
- patches: bfloat16 [32768, 1280], P(('dp', 'sp')), parts along dimension 0
- embeds: bfloat16 [16384, 2560], P(('dp', 'sp')), parts along dimension 0
- dest_slot: int32 [8192], P(('dp', 'sp')), parts along dimension 0
- rope_pos: int32 [3, 16384], P(None, ('dp', 'sp')), parts along dimension 1
- cu_doc: int32 [20], P('dp'), parts along dimension 0
- ln_w: bfloat16 [1280], replicated
- ln_b: bfloat16 [1280], replicated
- w_one: bfloat16 [5120, 5120], replicated
- b_one: bfloat16 [5120], replicated
- w_two: bfloat16 [5120, 2560], replicated
- b_two: bfloat16 [2560], replicated
- norm_attn: bfloat16 [2560], replicated
- w_q: bfloat16 [2560, 2560], replicated
- b_q: bfloat16 [2560], replicated
- w_k: bfloat16 [2560, 2560], replicated
- b_k: bfloat16 [2560], replicated
- w_v: bfloat16 [2560, 2560], replicated
- b_v: bfloat16 [2560], replicated
- w_o: bfloat16 [2560, 2560], replicated
- norm_mlp: bfloat16 [2560], replicated
- w_gate: bfloat16 [2560, 6912], replicated
- w_up: bfloat16 [2560, 6912], replicated
- w_down: bfloat16 [6912, 2560], replicated
Outputs:
- output: bfloat16 [16384, 2560], P(('dp', 'sp')), parts along dimension 0
There are 4 independent parts. A program takes and returns all parts, laid end to end along the dimension named above; an argument that names none is the same for every part.
All inputs are finite; a program needn't handle non-finite values.
Results may differ from a plain program's by a relative error of at most 0.0107878.
Values are sent between devices in bfloat16 or wider.
A program may use at most 768 MiB of HBM per device.

v0:
```python
import functools

import jax
import jax.numpy as jnp
from jax import lax
from jax.experimental import pallas as pl
from jax.experimental.pallas import tpu as pltpu
from jax.sharding import PartitionSpec as P

HEAD_DIM = 128
NORM_EPS = 1e-6
ROPE_THETA = 1000000.0
MROPE_SPLIT = (16, 40)
MESH = pl.DeviceIdType.MESH
VMEM_LIMIT = 60 * 1024 * 1024


def layer_norm(values_in, gain_vec, shift_vec):
    widened = values_in.astype(jnp.float32)
    centered = widened - jnp.mean(widened, axis=-1, keepdims=True)
    spread = jnp.mean(centered * centered, axis=-1, keepdims=True)
    return (centered * lax.rsqrt(spread + NORM_EPS) * gain_vec.astype(jnp.float32) + shift_vec.astype(jnp.float32)).astype(jnp.bfloat16)


def rms_norm(values_in, gain_vec):
    widened = values_in.astype(jnp.float32)
    return (widened * lax.rsqrt(jnp.mean(widened * widened, axis=-1, keepdims=True) + NORM_EPS) * gain_vec.astype(jnp.float32)).astype(jnp.bfloat16)


def merger_mlp(grouped, w_one, b_one, w_two, b_two):
    inner = jax.nn.gelu(jnp.dot(grouped, w_one, preferred_element_type=jnp.float32) + b_one.astype(jnp.float32), approximate=False).astype(jnp.bfloat16)
    return (jnp.dot(inner, w_two, preferred_element_type=jnp.float32) + b_two.astype(jnp.float32)).astype(jnp.bfloat16)


def rope_tables(rope_pos):
    inv_freq = ROPE_THETA ** (-jnp.arange(0, HEAD_DIM, 2, dtype=jnp.float32) / HEAD_DIM)
    freq_idx = jnp.arange(HEAD_DIM // 2)[None, :]
    chosen = jnp.where(freq_idx < MROPE_SPLIT[0], rope_pos[0][:, None], jnp.where(freq_idx < MROPE_SPLIT[1], rope_pos[1][:, None], rope_pos[2][:, None]))
    angles = chosen.astype(jnp.float32) * inv_freq[None, :]
    cos_h, sin_h = jnp.cos(angles), jnp.sin(angles)
    return jnp.concatenate([cos_h, cos_h], axis=-1), jnp.concatenate([-sin_h, sin_h], axis=-1)


def first_head(dev, group, heads):
    return (dev * heads + group - 1) // group


def owner_of(head, group, heads):
    return head * group // heads


def greet_group(group, me):
    barrier = pltpu.get_barrier_semaphore()
    for k in range(1, group):
        pl.semaphore_signal(barrier, inc=1, device_id={"sp": lax.rem(me + k, group)}, device_id_type=MESH)
    pl.semaphore_wait(barrier, group - 1)


def qkv_send_kernel(group, heads, a_ref, cos_ref, sin_ref, bias_ref, wq_ref, wk_ref, wv_ref, out_ref, wbuf, stage, w_sem, send_sem, recv_sem, own_sem):
    me = lax.axis_index("sp")
    depth = wbuf.shape[0]
    half = heads // 2
    mine = first_head(me, group, heads)

    def head_at(p):
        step = p // 2
        delta = step - (p % 2) * (2 * step + 1)
        return (mine + half + delta + heads) % heads

    def weight_copies(p):
        cols = pl.ds(pl.multiple_of(head_at(p) * HEAD_DIM, HEAD_DIM), HEAD_DIM)
        slot = p % depth
        return [
            pltpu.make_async_copy(w.at[:, cols], wbuf.at[slot, :, pl.ds(n * HEAD_DIM, HEAD_DIM)], w_sem.at[slot, n])
            for n, w in enumerate((wq_ref, wk_ref, wv_ref))
        ]

    def remote(p):
        head = head_at(p)
        target = owner_of(head, group, heads)
        slot = head - first_head(target, group, heads)
        copy = pltpu.make_async_remote_copy(
            src_ref=stage.at[p],
            dst_ref=out_ref.at[slot, :, me],
            send_sem=send_sem.at[p],
            recv_sem=recv_sem.at[slot],
            device_id={"sp": target},
            device_id_type=MESH,
        )
        local = pltpu.make_async_copy(stage.at[p], out_ref.at[slot, :, me], own_sem.at[slot])
        return target, copy, local

    def send(p):
        target, copy, local = remote(p)

        @pl.when(target != me)
        def _():
            copy.start()

        @pl.when(target == me)
        def _():
            local.start()

    for p in range(depth - 1):
        for c in weight_copies(p):
            c.start()
    greet_group(group, me)

    def step(p, carry):
        @pl.when(p + depth - 1 < heads)
        def _():
            for c in weight_copies(p + depth - 1):
                c.start()

        for c in weight_copies(p):
            c.wait()
        lin = jnp.dot(a_ref[...], wbuf[p % depth], preferred_element_type=jnp.float32) + bias_ref[head_at(p)]

        @pl.when(p > 0)
        def _():
            send(p - 1)

        cos_t, sin_t = cos_ref[...], sin_ref[...]
        for n in range(3):
            part = lin[:, n * HEAD_DIM:(n + 1) * HEAD_DIM]
            if n < 2:
                part = part * cos_t + pltpu.roll(part, HEAD_DIM // 2, 1) * sin_t
            stage[p, n] = part.astype(jnp.bfloat16)
        return carry

    lax.fori_loop(0, heads, step, 0)
    send(heads - 1)

    def drain(p, carry):
        target, copy, local = remote(p)

        @pl.when(target != me)
        def _():
            copy.wait_send()

        @pl.when(target == me)
        def _():
            local.wait()

        return carry

    lax.fori_loop(0, heads, drain, 0)
    count = first_head(me + 1, group, heads) - mine
    for slot in range(out_ref.shape[0]):
        landed = out_ref.at[slot, :, pl.ds(0, group - 1)]

        @pl.when(slot < count)
        def _():
            pltpu.make_async_copy(landed, landed, recv_sem.at[slot]).wait()


def qkv_send(group, heads, normed, cos_t, sin_t, biases, w_q, w_k, w_v):
    tokens, width = normed.shape
    slots = -(-heads // group)
    vmem = pl.BlockSpec(memory_space=pltpu.VMEM)
    hbm = pl.BlockSpec(memory_space=pl.ANY)
    return pl.pallas_call(
        functools.partial(qkv_send_kernel, group, heads),
        out_shape=jax.ShapeDtypeStruct((slots, 3, group, tokens, HEAD_DIM), jnp.bfloat16),
        in_specs=[vmem, vmem, vmem, vmem, hbm, hbm, hbm],
        out_specs=hbm,
        scratch_shapes=[
            pltpu.VMEM((3, width, 3 * HEAD_DIM), jnp.bfloat16),
            pltpu.VMEM((heads, 3, tokens, HEAD_DIM), jnp.bfloat16),
            pltpu.SemaphoreType.DMA((3, 3)),
            pltpu.SemaphoreType.DMA((heads,)),
            pltpu.SemaphoreType.DMA((slots,)),
            pltpu.SemaphoreType.DMA((slots,)),
        ],
        compiler_params=pltpu.CompilerParams(collective_id=0, has_side_effects=True, vmem_limit_bytes=VMEM_LIMIT),
        cost_estimate=pl.CostEstimate(flops=2 * tokens * width * 3 * heads * HEAD_DIM, bytes_accessed=3 * width * heads * HEAD_DIM * 2, transcendentals=0),
        name="qkv_send",
    )(normed, cos_t, sin_t, biases, w_q, w_k, w_v)


def attention_kernel(q_rows, k_rows, cuts, info_ref, q_ref, k_ref, v_ref, o_ref):
    slots = q_ref.shape[0]
    start = pl.program_id(0) * q_rows
    low, high = 0, 0
    for d in range(cuts):
        low = jnp.where(start >= info_ref[1 + d], info_ref[1 + d], low)
        high = jnp.where(start + q_rows - 1 >= info_ref[1 + d], info_ref[1 + d], high)
    q_pos = start + lax.broadcasted_iota(jnp.int32, (q_rows, 1), 0)
    q_low = jnp.zeros((q_rows, 1), jnp.int32)
    for d in range(cuts):
        q_low = jnp.where(q_pos >= info_ref[1 + d], info_ref[1 + d], q_low)
    scale = HEAD_DIM ** -0.5 * 1.4426950408889634
    first = low // k_rows
    diag = start // k_rows
    inner = jnp.minimum((high + k_rows - 1) // k_rows, diag)
    last = (start + q_rows - 1) // k_rows

    def run(heads):
        def step(masked, j, carry):
            rows = pl.ds(pl.multiple_of(j * k_rows, k_rows), k_rows)
            if masked:
                k_pos = j * k_rows + lax.broadcasted_iota(jnp.int32, (1, k_rows), 1)
                seen = (k_pos <= q_pos) & (k_pos >= q_low)
            scores, out = [], []
            for h in range(heads):
                s = lax.dot_general(q_ref[h], k_ref[h, rows, :], (((1,), (1,)), ((), ())), preferred_element_type=jnp.float32)
                scores.append(jnp.where(seen, s, -1e30) if masked else s)
            for h in range(heads):
                top, total, acc = carry[h]
                new_top = jnp.maximum(top, jnp.max(scores[h], axis=1, keepdims=True))
                decay = jnp.exp2((top - new_top) * scale)
                probs = jnp.exp2((scores[h] - new_top) * scale)
                total = total * decay + jnp.sum(probs, axis=1, keepdims=True)
                acc = acc * decay + jnp.dot(probs.astype(jnp.bfloat16), v_ref[h, rows, :], preferred_element_type=jnp.float32)
                out.append((new_top, total, acc))
            return tuple(out)

        carry = tuple((jnp.full((q_rows, 1), -1e30, jnp.float32), jnp.zeros((q_rows, 1), jnp.float32), jnp.zeros((q_rows, HEAD_DIM), jnp.float32)) for _ in range(heads))
        carry = lax.fori_loop(first, inner, functools.partial(step, True), carry)
        carry = lax.fori_loop(inner, diag, functools.partial(step, False), carry)
        carry = lax.fori_loop(diag, last + 1, functools.partial(step, True), carry)
        for h in range(heads):
            _, total, acc = carry[h]
            o_ref[h] = (acc / total).astype(jnp.bfloat16)

    for heads in range(1, slots + 1):
        pl.when(info_ref[0] == heads)(functools.partial(run, heads))


def attention(info, qkv, cuts, q_rows, k_rows):
    slots, _, group, tokens, _ = qkv.shape
    seq = group * tokens
    flat = qkv.reshape(slots, 3, seq, HEAD_DIM)

    def whole(part):
        return pl.BlockSpec((slots, None, seq, HEAD_DIM), lambda i, info: (0, part, 0, 0))

    return pl.pallas_call(
        functools.partial(attention_kernel, q_rows, k_rows, cuts),
        grid_spec=pltpu.PrefetchScalarGridSpec(
            num_scalar_prefetch=1,
            grid=(seq // q_rows,),
            in_specs=[pl.BlockSpec((slots, None, q_rows, HEAD_DIM), lambda i, info: (0, 0, i, 0)), whole(1), whole(2)],
            out_specs=pl.BlockSpec((slots, q_rows, HEAD_DIM), lambda i, info: (0, i, 0)),
        ),
        out_shape=jax.ShapeDtypeStruct((slots, seq, HEAD_DIM), jnp.bfloat16),
        compiler_params=pltpu.CompilerParams(vmem_limit_bytes=VMEM_LIMIT),
        cost_estimate=pl.CostEstimate(flops=4 * seq * seq * HEAD_DIM, bytes_accessed=8 * seq * HEAD_DIM * slots, transcendentals=seq * seq // 2),
        name="attention",
    )(info, flat, flat, flat).reshape(slots, group, tokens, HEAD_DIM)


def out_send_kernel(group, heads, o_ref, attn_ref, send_sem, recv_sem, own_sem):
    me = lax.axis_index("sp")
    mine = first_head(me, group, heads)
    count = first_head(me + 1, group, heads) - mine
    slots = o_ref.shape[0]
    greet_group(group, me)

    def hop(k):
        step = k // 2
        return (me + group // 2 + step - (k % 2) * (2 * step + 1) + group) % group

    def out_copy(slot, k):
        head = mine + slot
        return pltpu.make_async_remote_copy(
            src_ref=o_ref.at[slot, hop(k)],
            dst_ref=attn_ref.at[head],
            send_sem=send_sem.at[slot, k],
            recv_sem=recv_sem.at[head],
            device_id={"sp": hop(k)},
            device_id_type=MESH,
        )

    def own_copy(slot):
        return pltpu.make_async_copy(o_ref.at[slot, me], attn_ref.at[mine + slot], own_sem.at[slot])

    for slot in range(slots):

        @pl.when(slot < count)
        def _():
            for k in range(group - 1):
                out_copy(slot, k).start()
            own_copy(slot).start()

    for slot in range(slots):

        @pl.when(slot < count)
        def _():
            for k in range(group - 1):
                out_copy(slot, k).wait_send()
            own_copy(slot).wait()

    def landed(head, carry):
        @pl.when(owner_of(head, group, heads) != me)
        def _():
            block = attn_ref.at[head]
            pltpu.make_async_copy(block, block, recv_sem.at[head]).wait()

        return carry

    lax.fori_loop(0, heads, landed, 0)


def out_send(group, heads, o_heads):
    slots, _, tokens, _ = o_heads.shape
    hbm = pl.BlockSpec(memory_space=pl.ANY)
    return pl.pallas_call(
        functools.partial(out_send_kernel, group, heads),
        out_shape=jax.ShapeDtypeStruct((heads, tokens, HEAD_DIM), jnp.bfloat16),
        in_specs=[pl.BlockSpec(memory_space=pltpu.VMEM)],
        out_specs=hbm,
        scratch_shapes=[
            pltpu.SemaphoreType.DMA((slots, group - 1)),
            pltpu.SemaphoreType.DMA((heads,)),
            pltpu.SemaphoreType.DMA((slots,)),
        ],
        compiler_params=pltpu.CompilerParams(collective_id=1, has_side_effects=True),
        name="out_send",
    )(o_heads)


def place_rows_kernel(group, pieces, merged_ref, slots_ref, embeds_ref, gain_ref, h_ref, a_ref, rows, slots, total, hits, slot_send, slot_recv, ring_send, ring_recv, pair_send, pair_recv):
    me = lax.axis_index("sp")
    core = me % 2
    way = 2 - 4 * core
    ahead = (me + way + group) % group
    other = me + 1 - 2 * core
    hops = group // 2
    count = merged_ref.shape[0] // pieces
    greet_group(group, me)

    def origin(dev, step):
        return (dev - (2 - 4 * (dev % 2)) * step + 2 * group * group) % group

    def slot_copy(k):
        return pltpu.make_async_remote_copy(
            src_ref=slots_ref, dst_ref=slots.at[me], send_sem=slot_send.at[k], recv_sem=slot_recv.at[me],
            device_id={"sp": lax.rem(me + k, group)}, device_id_type=MESH,
        )

    def block(ref, step, piece):
        return ref.at[origin(me, step), pl.ds(piece * count, count)]

    def source(step, piece):
        return merged_ref.at[pl.ds(piece * count, count)] if step == 0 else block(rows, step, piece)

    def ring_copy(step, piece):
        return pltpu.make_async_remote_copy(
            src_ref=source(step, piece), dst_ref=block(rows, step, piece), send_sem=ring_send.at[step, piece],
            recv_sem=ring_recv.at[step, piece], device_id={"sp": ahead}, device_id_type=MESH,
        )

    def pair_copy(step, piece):
        return pltpu.make_async_remote_copy(
            src_ref=source(step, piece), dst_ref=block(rows, step, piece), send_sem=pair_send.at[step, piece],
            recv_sem=pair_recv.at[step, piece], device_id={"sp": other}, device_id_type=MESH,
        )

    for k in range(1, group):
        slot_copy(k).start()
    for piece in range(pieces):
        ring_copy(0, piece).start()
        pair_copy(0, piece).start()
    slots[me] = slots_ref[...]
    total[...] = jnp.zeros_like(total)
    hits[...] = jnp.zeros_like(hits)
    tokens = embeds_ref.shape[0]

    def place(dev, values):
        wanted = me * tokens + lax.broadcasted_iota(jnp.int32, (tokens, 1), 0)
        pick = jnp.where(slots[dev] == wanted, 1.0, 0.0)
        hits[...] += pick
        total[...] += jnp.dot(pick.astype(jnp.bfloat16), values, preferred_element_type=jnp.float32)

    for k in range(1, group):
        dev = lax.rem(me + k, group)
        pltpu.make_async_copy(slots.at[dev], slots.at[dev], slot_recv.at[dev]).wait()
    place(me, merged_ref[...])
    for step in range(hops):
        if step > 0:
            for piece in range(pieces):
                landed = block(rows, step, piece)
                pltpu.make_async_copy(landed, landed, ring_recv.at[step - 1, piece]).wait()
                if step < hops - 1:
                    ring_copy(step, piece).start()
                pair_copy(step, piece).start()
            place(origin(me, step), rows[origin(me, step)])
        theirs = origin(other, step)
        for piece in range(pieces):
            landed = rows.at[theirs, pl.ds(piece * count, count)]
            pltpu.make_async_copy(landed, landed, pair_recv.at[step, piece]).wait()
        place(theirs, rows[theirs])
    found = jnp.max(hits[...], axis=1, keepdims=True) > 0.0
    h_zero = jnp.where(found, total[...].astype(jnp.bfloat16), embeds_ref[...])
    h_ref[...] = h_zero
    a_ref[...] = rms_norm(h_zero, gain_ref[...])
    for k in range(1, group):
        slot_copy(k).wait_send()
    for step in range(hops):
        for piece in range(pieces):
            if step < hops - 1:
                ring_copy(step, piece).wait_send()
            pair_copy(step, piece).wait_send()


def place_rows(group, merged, dest_slot, embeds, gain):
    rows, width = merged.shape
    tokens = embeds.shape[0]
    pieces = 4
    hops = group // 2
    vmem = pl.BlockSpec(memory_space=pltpu.VMEM)
    out = jax.ShapeDtypeStruct((tokens, width), jnp.bfloat16)
    return pl.pallas_call(
        functools.partial(place_rows_kernel, group, pieces),
        out_shape=(out, out),
        in_specs=[vmem] * 4,
        out_specs=(vmem, vmem),
        scratch_shapes=[
            pltpu.VMEM((group, rows, width), jnp.bfloat16),
            pltpu.VMEM((group, 1, rows), jnp.int32),
            pltpu.VMEM((tokens, width), jnp.float32),
            pltpu.VMEM((tokens, rows), jnp.float32),
            pltpu.SemaphoreType.DMA((group,)),
            pltpu.SemaphoreType.DMA((group,)),
            pltpu.SemaphoreType.DMA((hops, pieces)),
            pltpu.SemaphoreType.DMA((hops, pieces)),
            pltpu.SemaphoreType.DMA((hops, pieces)),
            pltpu.SemaphoreType.DMA((hops, pieces)),
        ],
        compiler_params=pltpu.CompilerParams(collective_id=2, has_side_effects=True, vmem_limit_bytes=VMEM_LIMIT),
        name="place_rows",
    )(merged, dest_slot.reshape(1, rows), embeds, gain.reshape(1, width))


def mlp_kernel(o_cols, chunk, attn_ref, h_ref, gain_ref, wo_ref, wg_ref, wu_ref, wd_ref, out_ref, attn, h_one, normed, total, wo, wg, wu, wd, o_sem, f_sem):
    heads, _, dim = attn_ref.shape
    width = h_ref.shape[1]
    o_steps, steps = width // o_cols, wg_ref.shape[1] // chunk

    def o_copy(i):
        return pltpu.make_async_copy(wo_ref.at[:, pl.ds(i * o_cols, o_cols)], wo.at[i % 2], o_sem.at[i % 2])

    def f_copies(i):
        b = i % 2
        cols = pl.ds(pl.multiple_of(i * chunk, 128), chunk)
        return [
            pltpu.make_async_copy(wg_ref.at[:, cols], wg.at[b], f_sem.at[b, 0]),
            pltpu.make_async_copy(wu_ref.at[:, cols], wu.at[b], f_sem.at[b, 1]),
            pltpu.make_async_copy(wd_ref.at[cols, :], wd.at[b], f_sem.at[b, 2]),
        ]

    o_copy(0).start()
    o_copy(1).start()
    for h in range(heads):
        attn[:, h * dim:(h + 1) * dim] = attn_ref[h]
    for i in range(o_steps):
        o_copy(i).wait()
        cols = slice(i * o_cols, (i + 1) * o_cols)
        part = jnp.dot(attn[...], wo[i % 2], preferred_element_type=jnp.float32)
        h_one[:, cols] = (h_ref[:, cols].astype(jnp.float32) + part).astype(jnp.bfloat16)
        if i + 2 < o_steps:
            o_copy(i + 2).start()
        if i == o_steps - 3:
            for c in f_copies(0):
                c.start()
    normed[...] = rms_norm(h_one[...], gain_ref[...])
    total[...] = h_one[...].astype(jnp.float32)

    def step(i, carry):
        b = i % 2

        @pl.when(i + 1 < steps)
        def _():
            for c in f_copies(i + 1):
                c.start()

        gate_copy, up_copy, down_copy = f_copies(i)
        gate_copy.wait()
        up_copy.wait()
        gate_pre = jnp.dot(normed[...], wg[b], preferred_element_type=jnp.float32)
        up_pre = jnp.dot(normed[...], wu[b], preferred_element_type=jnp.float32)
        activated = (jax.nn.silu(gate_pre) * up_pre).astype(jnp.bfloat16)
        down_copy.wait()
        total[...] += jnp.dot(activated, wd[b], preferred_element_type=jnp.float32)
        return carry

    lax.fori_loop(0, steps, step, 0)
    out_ref[...] = total[...].astype(jnp.bfloat16)


def mlp(attn, h_zero, gain, w_o, w_gate, w_up, w_down):
    heads, tokens, dim = attn.shape
    width, ffn = w_gate.shape
    o_cols = width // 5
    chunk = ffn // 9
    vmem = pl.BlockSpec(memory_space=pltpu.VMEM)
    hbm = pl.BlockSpec(memory_space=pl.ANY)
    return pl.pallas_call(
        functools.partial(mlp_kernel, o_cols, chunk),
        out_shape=jax.ShapeDtypeStruct((tokens, width), jnp.bfloat16),
        in_specs=[vmem, vmem, vmem, hbm, hbm, hbm, hbm],
        out_specs=vmem,
        scratch_shapes=[
            pltpu.VMEM((tokens, heads * dim), jnp.bfloat16),
            pltpu.VMEM((tokens, width), jnp.bfloat16),
            pltpu.VMEM((tokens, width), jnp.bfloat16),
            pltpu.VMEM((tokens, width), jnp.float32),
            pltpu.VMEM((2, heads * dim, o_cols), jnp.bfloat16),
            pltpu.VMEM((2, width, chunk), jnp.bfloat16),
            pltpu.VMEM((2, width, chunk), jnp.bfloat16),
            pltpu.VMEM((2, chunk, width), jnp.bfloat16),
            pltpu.SemaphoreType.DMA((2,)),
            pltpu.SemaphoreType.DMA((2, 3)),
        ],
        compiler_params=pltpu.CompilerParams(vmem_limit_bytes=VMEM_LIMIT),
        cost_estimate=pl.CostEstimate(flops=2 * tokens * width * (3 * ffn + width), bytes_accessed=2 * width * (3 * ffn + width), transcendentals=tokens * ffn),
        name="mlp",
    )(attn, h_zero, gain.reshape(1, width), w_o, w_gate, w_up, w_down)


def solution(mesh):
    group = mesh.shape['sp']
    row_spec = P(('dp', 'sp'), None)

    def local_step(patches, embeds, dest_slot, rope_pos, cu_doc, ln_w, ln_b, w_one, b_one, w_two, b_two, norm_attn, w_q, b_q, w_k, b_k, w_v, b_v, w_o, norm_mlp, w_gate, w_up, w_down):
        tok_dev = embeds.shape[0]
        merged_dev = dest_slot.shape[0]
        heads = w_q.shape[1] // HEAD_DIM
        me = lax.axis_index('sp')
        normed = layer_norm(patches, ln_w, ln_b).reshape(merged_dev, -1)
        merged = merger_mlp(normed, w_one, b_one, w_two, b_two)
        h_zero, normed_a = place_rows(group, merged, dest_slot, embeds, norm_attn)
        cos_t, sin_t = rope_tables(rope_pos)
        biases = jnp.concatenate([b.astype(jnp.float32).reshape(heads, 1, HEAD_DIM) for b in (b_q, b_k, b_v)], axis=2)
        qkv = qkv_send(group, heads, normed_a, cos_t, sin_t, biases, w_q, w_k, w_v)
        count = first_head(me + 1, group, heads) - first_head(me, group, heads)
        cuts = cu_doc.shape[0] - 2
        info = jnp.concatenate([count.astype(jnp.int32).reshape(1), cu_doc[1:-1]])
        o_heads = attention(info, qkv, cuts, 512, 512)
        attn_out = out_send(group, heads, o_heads)
        return mlp(attn_out, h_zero, norm_mlp, w_o, w_gate, w_up, w_down)

    in_specs = (row_spec, row_spec, P(('dp', 'sp')), P(None, ('dp', 'sp')), P('dp')) + (P(),) * 18
    return jax.shard_map(local_step, mesh=mesh, in_specs=in_specs, out_specs=row_spec, check_vma=False)
```

profile of v0, /device:TPU:60, one launch (start us, length us, event | category | flops | bytes accessed | tf_op | source)
XLA Modules:
  0.0 339.9 jit_solution(9371693966713595092)
XLA Ops:
  0.0 0.8 slice.12
  0.8 0.6 pad_add_fusion.info_ref
  1.5 0.8 fusion.82
  2.3 0.6 fusion.51
  2.9 0.8 pad_maximum_fusion
  3.8 1.6 convert_reduce_fusion
  5.3 0.0 copy-done
  5.3 0.5 fusion.3
  5.8 0.0 copy-done.8
  5.9 0.0 copy-done.9
  5.9 0.0 copy-start.1
  5.9 0.0 copy-start.2
  5.9 0.6 fusion.6
  6.5 0.8 reshape.70
  7.3 0.0 copy-done.1
  7.3 0.0 copy-done.2
  7.4 0.0 copy-start.3
  7.4 0.0 copy-start.4
  7.4 0.0 copy-start.5
  7.4 0.0 copy-start.6
  7.4 29.6 %fusion.merged_ref = bf16[128,2560]{1,0:T(8,128)(2,1)} fusion(bf16[5120,2560]{1,0:T(8,128)(2,1)} %param.32, bf16[128,5120]{1,0:T(8,128)(2,1)S(1)} %reshape.70, bf16[5120,5120]{1,0:T(8,128)(2,1)} %param.30, f32[5120]{0:T(1024)S(1)} %convert_element_type.34, f32[2560]{0:T(1024)S(1)} %convert_element_type.36), kind=kOutput, calls=%fused_computation.3 | convolution fusion | flops 10110238720 | bytes 80640000 | tf_op jit(solution)/shard_map/dot_general | solution.py:32
  37.0 0.0 copy-done.3
  37.0 0.6 reshape.72.gain_ref
  37.6 65.3 %place_rows.1 = (bf16[256,2560]{1,0:T(8,128)(2,1)}, bf16[256,2560]{1,0:T(8,128)(2,1)}) custom-call(bf16[128,2560]{1,0:T(8,128)(2,1)} %fusion.merged_ref, s32[1,128]{1,0:T(1,128)} %bitcast.23, bf16[256,2560]{1,0:T(8,128)(2,1)} %embeds_ref.1, bf16[1,2560]{1,0:T(2,128)(2,1)} %reshape.72.gain_ref), custom_call_target="tpu_custom_call" | custom-call | tf_op jit(solution)/shard_map/place_rows/pallas_call | solution.py:414
  102.9 0.0 copy-done.4
  102.9 0.0 copy-done.5
  103.0 0.6 maximum_convert_fusion.bias_ref
  103.6 101.2 %qkv_send.1 = bf16[2,3,16,256,128]{4,3,2,1,0:T(8,128)(2,1)} custom-call(bf16[256,2560]{1,0:T(8,128)(2,1)} %get-tuple-element.7.a_ref, f32[256,128]{1,0:T(8,128)} %get-tuple-element.15.cos_ref, f32[256,128]{1,0:T(8,128)} %get-tuple-element.16.sin_ref, f32[20,1,384]{2,1,0:T(1,128)} %maximum_convert_fusion.bias_ref, bf16[2560,2560]{1,0:T(8,128)(2,1)} %wq_ref.1, ...), custom_call_target="tpu_custom_call" | custom-call | flops 10066329600 | bytes 39321600 | tf_op jit(solution)/shard_map/qkv_send/pallas_call | solution.py:162
  204.8 29.2 %attention.1 = bf16[2,4096,128]{2,1,0:T(8,128)(2,1)} custom-call(s32[4]{0:T(128)} %pad_add_fusion.info_ref, bf16[2,3,4096,128]{3,2,1,0:T(8,128)(2,1)} %bitcast.13, bf16[2,3,4096,128]{3,2,1,0:T(8,128)(2,1)} %bitcast.14, bf16[2,3,4096,128]{3,2,1,0:T(8,128)(2,1)} %bitcast.15), custom_call_target="tpu_custom_call" | custom-call | flops 8589934592 | bytes 8388608 | tf_op jit(solution)/shard_map/attention/pallas_call | solution.py:238
  234.0 60.5 %out_send.1.attn_ref = bf16[20,256,128]{2,1,0:T(8,128)(2,1)} custom-call(bf16[2,16,256,128]{3,2,1,0:T(8,128)(2,1)} %bitcast.16), custom_call_target="tpu_custom_call" | custom-call | tf_op jit(solution)/shard_map/out_send/pallas_call | solution.py:308
  294.5 0.6 reshape.78.gain_ref
  295.1 44.6 %mlp.1 = bf16[256,2560]{1,0:T(8,128)(2,1)} custom-call(bf16[20,256,128]{2,1,0:T(8,128)(2,1)} %out_send.1.attn_ref, bf16[256,2560]{1,0:T(8,128)(2,1)} %get-tuple-element.8.h_ref, bf16[1,2560]{1,0:T(2,128)(2,1)} %reshape.78.gain_ref, bf16[2560,2560]{1,0:T(8,128)(2,1)} %wo_ref.1, bf16[2560,6912]{1,0:T(8,128)(2,1)} %wg_ref.1, bf16[2560,6912]{1,0:T(8,128)(2,1)} %wu_ref.1, ...), custom_call_target="tpu_custom_call" | custom-call | flops 30534533120 | bytes 119275520 | tf_op jit(solution)/shard_map/mlp/pallas_call | solution.py:499
  (18 shorter events, 0.1 us)
Async XLA Ops:
  0.0 5.3 %copy-start = (bf16[512,1280]{1,0:T(8,128)(2,1)S(1)}, bf16[512,1280]{1,0:T(8,128)(2,1)}, u32[]{:S(2)}) copy-start(bf16[512,1280]{1,0:T(8,128)(2,1)} %param.23) | copy-start | bytes 3932164
  0.0 5.8 %copy-start.8 = (bf16[1280]{0:T(1024)(128)(2,1)S(1)}, bf16[1280]{0:T(1024)(128)(2,1)}, u32[]{:S(2)}) copy-start(bf16[1280]{0:T(1024)(128)(2,1)} %param.28) | copy-start | bytes 7684
  0.0 5.9 %copy-start.9 = (bf16[1280]{0:T(1024)(128)(2,1)S(1)}, bf16[1280]{0:T(1024)(128)(2,1)}, u32[]{:S(2)}) copy-start(bf16[1280]{0:T(1024)(128)(2,1)} %param.29) | copy-start | bytes 7684
  5.9 1.4 copy-start.1
  5.9 1.4 copy-start.2
  7.4 29.6 %copy-start.3 = (bf16[2560]{0:T(1024)(128)(2,1)S(1)}, bf16[2560]{0:T(1024)(128)(2,1)}, u32[]{:S(2)}) copy-start(bf16[2560]{0:T(1024)(128)(2,1)} %param.34) | copy-start | bytes 15364
  7.4 95.6 %copy-start.4 = (bf16[2560]{0:T(1024)(128)(2,1)S(1)}, bf16[2560]{0:T(1024)(128)(2,1)}, u32[]{:S(2)}) copy-start(bf16[2560]{0:T(1024)(128)(2,1)} %param.36) | copy-start | bytes 15364
  7.4 95.6 %copy-start.5 = (bf16[2560]{0:T(1024)(128)(2,1)S(1)}, bf16[2560]{0:T(1024)(128)(2,1)}, u32[]{:S(2)}) copy-start(bf16[2560]{0:T(1024)(128)(2,1)} %param.38) | copy-start | bytes 15364
  7.4 95.6 %copy-start.6 = (bf16[2560]{0:T(1024)(128)(2,1)S(1)}, bf16[2560]{0:T(1024)(128)(2,1)}, u32[]{:S(2)}) copy-start(bf16[2560]{0:T(1024)(128)(2,1)} %param.40) | copy-start | bytes 15364
  234.0 60.5 %copy-start.7 = (bf16[2560]{0:T(1024)(128)(2,1)S(1)}, bf16[2560]{0:T(1024)(128)(2,1)}, u32[]{:S(2)}) copy-start(bf16[2560]{0:T(1024)(128)(2,1)} %param.42) | copy-start | bytes 15364
where the time goes:
time: 338 us; the launch traced here: 340 us
  Pallas kernels  301 us (89%)
  matrix products  29.6 us (9%)
  other arithmetic  5.37 us (2%)
  local copies, waits for them, and re-layouts  3.75 us (1%)
    pallas_call x1, Pallas kernels, qkv_send(): pl.pallas_call(functools.partial(qkv_send_kernel, group, heads), out_shap...  101 us
    pallas_call x1, Pallas kernels, place_rows(): pl.pallas_call(functools.partial(place_rows_kernel, group, pieces), out_s...  65.3 us
    pallas_call x1, Pallas kernels, out_send(): pl.pallas_call(functools.partial(out_send_kernel, group, heads), out_shap...  60.5 us
    pallas_call x1, Pallas kernels, mlp(): pl.pallas_call(functools.partial(mlp_kernel, o_cols, chunk), out_shape=ja...  44.6 us
    dot_general x1, matrix products, merger_mlp(): jnp.dot(inner, w_two, preferred_element_type=jnp.float32)  29.6 us
    pallas_call x1, Pallas kernels, attention(): pl.pallas_call(functools.partial(attention_kernel, q_rows, k_rows, cuts),...  29.2 us

commit v1 on v0

--- a/solution.py
+++ b/solution.py
@@ -56,16 +56,20 @@
     pl.semaphore_wait(barrier, group - 1)
 
 
-def qkv_send_kernel(group, heads, a_ref, cos_ref, sin_ref, bias_ref, wq_ref, wk_ref, wv_ref, out_ref, wbuf, stage, w_sem, send_sem, recv_sem, own_sem):
+def mixer_kernel(group, heads, cuts, cu_ref, a_ref, cos_ref, sin_ref, bias_ref, wq_ref, wk_ref, wv_ref, attn_ref, wbuf, stage, land, top_ref, sum_ref, acc_ref, o_ref, w_sem, send_sem, recv_sem, own_sem, o_send, o_recv, o_own):
     me = lax.axis_index("sp")
+    chips = group // 2
+    my_chip = me // 2
     depth = wbuf.shape[0]
-    half = heads // 2
+    slots = land.shape[0]
+    tokens = a_ref.shape[0]
+    rows = 2 * tokens
     mine = first_head(me, group, heads)
+    count = first_head(me + 1, group, heads) - mine
 
     def head_at(p):
-        step = p // 2
-        delta = step - (p % 2) * (2 * step + 1)
-        return (mine + half + delta + heads) % heads
+        step = (p + 1) // 2
+        return (mine + (2 * (p % 2) - 1) * step + heads) % heads
 
     def weight_copies(p):
         cols = pl.ds(pl.multiple_of(head_at(p) * HEAD_DIM, HEAD_DIM), HEAD_DIM)
@@ -81,13 +85,13 @@
         slot = head - first_head(target, group, heads)
         copy = pltpu.make_async_remote_copy(
             src_ref=stage.at[p],
-            dst_ref=out_ref.at[slot, :, me],
+            dst_ref=land.at[slot, me],
             send_sem=send_sem.at[p],
-            recv_sem=recv_sem.at[slot],
+            recv_sem=recv_sem.at[slot, me],
             device_id={"sp": target},
             device_id_type=MESH,
         )
-        local = pltpu.make_async_copy(stage.at[p], out_ref.at[slot, :, me], own_sem.at[slot])
+        local = pltpu.make_async_copy(stage.at[p], land.at[slot, me], own_sem.at[slot])
         return target, copy, local
 
     def send(p):
@@ -106,7 +110,7 @@
             c.start()
     greet_group(group, me)
 
-    def step(p, carry):
+    def project(p, carry):
         @pl.when(p + depth - 1 < heads)
         def _():
             for c in weight_copies(p + depth - 1):
@@ -128,196 +132,213 @@
             stage[p, n] = part.astype(jnp.bfloat16)
         return carry
 
-    lax.fori_loop(0, heads, step, 0)
+    lax.fori_loop(0, heads, project, 0)
+
+    def clear(c, carry):
+        for slot in range(slots):
+            top_ref[slot, c] = jnp.full((rows, HEAD_DIM), -1e30, jnp.float32)
+            sum_ref[slot, c] = jnp.zeros((rows, HEAD_DIM), jnp.float32)
+            acc_ref[slot, c] = jnp.zeros((rows, HEAD_DIM), jnp.float32)
+        return carry
+
     send(heads - 1)
+    lax.fori_loop(0, chips, clear, 0)
+    scale = HEAD_DIM ** -0.5 * 1.4426950408889634
+
+    def chip_at(t):
+        step = (t + 1) // 2
+        return (my_chip + (2 * (t % 2) - 1) * step + chips) % chips
+
+    def block(slot, part, chip):
+        return land[slot, pl.ds(2 * chip, 2), part].reshape(rows, HEAD_DIM)
+
+    def attend(slot, q_chip, k_chip, causal):
+        scores = lax.dot_general(block(slot, 0, q_chip), block(slot, 1, k_chip), (((1,), (1,)), ((), ())), preferred_element_type=jnp.float32)
+        q_pos = q_chip * rows + lax.broadcasted_iota(jnp.int32, (rows, 1), 0)
+        q_low = jnp.zeros((rows, 1), jnp.int32)
+        for d in range(1, cuts + 1):
+            q_low = jnp.where(q_pos >= cu_ref[d], cu_ref[d], q_low)
+        k_pos = k_chip * rows + lax.broadcasted_iota(jnp.int32, (1, rows), 1)
+        seen = k_pos >= q_low
+        if causal:
+            seen = seen & (k_pos <= q_pos)
+        scores = jnp.where(seen, scores, -1e30)
+        top = top_ref[slot, q_chip]
+        new_top = jnp.maximum(top, jnp.max(scores, axis=1, keepdims=True))
+        decay = jnp.exp2((top - new_top) * scale)
+        total = sum_ref[slot, q_chip] * decay
+        parts = []
+        for n in range(rows // HEAD_DIM):
+            probs = jnp.exp2((scores[:, n * HEAD_DIM:(n + 1) * HEAD_DIM] - new_top) * scale)
+            total = total + probs
+            parts.append(probs.astype(jnp.bfloat16))
+        mixed = jnp.dot(jnp.concatenate(parts, axis=1), block(slot, 2, k_chip), preferred_element_type=jnp.float32)
+        top_ref[slot, q_chip] = new_top
+        sum_ref[slot, q_chip] = total
+        acc_ref[slot, q_chip] = acc_ref[slot, q_chip] * decay + mixed
+
+    def for_slots(action):
+        lax.fori_loop(0, count, lambda slot, carry: (action(slot), carry)[1], 0)
+
+    def wait_chip(chip):
+        def one(slot):
+            for core in range(2):
+                dev = 2 * chip + core
+                landed = land.at[slot, dev]
+
+                @pl.when(dev != me)
+                def _():
+                    pltpu.make_async_copy(landed, landed, recv_sem.at[slot, dev]).wait()
+
+                @pl.when(dev == me)
+                def _():
+                    pltpu.make_async_copy(landed, landed, own_sem.at[slot]).wait()
+
+        for_slots(one)
+
+    def pair(t, u):
+        here, there = chip_at(t), chip_at(u)
+        later = (here - there + chips) // chips
+        q_chip = here * later + there * (1 - later)
+        k_chip = there * later + here * (1 - later)
+        for_slots(lambda slot: attend(slot, q_chip, k_chip, False))
+
+    def o_copy(slot, dev):
+        return pltpu.make_async_remote_copy(
+            src_ref=o_ref.at[slot, dev],
+            dst_ref=attn_ref.at[mine + slot],
+            send_sem=o_send.at[slot, dev],
+            recv_sem=o_recv.at[mine + slot],
+            device_id={"sp": dev},
+            device_id_type=MESH,
+        )
+
+    def o_local(slot):
+        return pltpu.make_async_copy(o_ref.at[slot, me], attn_ref.at[mine + slot], o_own.at[slot])
+
+    def finish(chip):
+        def divide(slot):
+            total = jnp.sum(sum_ref[slot, chip], axis=1, keepdims=True)
+            out = (acc_ref[slot, chip] / total).astype(jnp.bfloat16)
+            o_ref[slot, pl.ds(2 * chip, 2)] = out.reshape(2, tokens, HEAD_DIM)
+
+        def give(slot):
+            for core in range(2):
+                dev = 2 * chip + core
+
+                @pl.when(dev != me)
+                def _():
+                    o_copy(slot, dev).start()
+
+                @pl.when(dev == me)
+                def _():
+                    o_local(slot).start()
+
+        for_slots(divide)
+        for_slots(give)
+
+    def arrival(t, carry):
+        chip = chip_at(t)
+        wait_chip(chip)
+        for_slots(lambda slot: attend(slot, chip, chip, True))
+        lax.fori_loop(0, t, lambda u, c: (pair(t, u), c)[1], 0)
+        return carry
+
+    last = chips - 1
+    far = chip_at(last)
+    lax.fori_loop(0, last, arrival, 0)
+
+    def early(u, carry):
+        @pl.when(chip_at(u) < far)
+        def _():
+            finish(chip_at(u))
+
+        return carry
+
+    lax.fori_loop(0, last, early, 0)
+    wait_chip(far)
+    for_slots(lambda slot: attend(slot, far, far, True))
+
+    def late(u, carry):
+        pair(last, u)
+
+        @pl.when(chip_at(u) > far)
+        def _():
+            finish(chip_at(u))
+
+        return carry
+
+    lax.fori_loop(0, last, late, 0)
+    finish(far)
 
     def drain(p, carry):
-        target, copy, local = remote(p)
+        target, copy, _ = remote(p)
 
         @pl.when(target != me)
         def _():
             copy.wait_send()
 
-        @pl.when(target == me)
-        def _():
-            local.wait()
-
         return carry
 
     lax.fori_loop(0, heads, drain, 0)
-    count = first_head(me + 1, group, heads) - mine
-    for slot in range(out_ref.shape[0]):
-        landed = out_ref.at[slot, :, pl.ds(0, group - 1)]
-
-        @pl.when(slot < count)
-        def _():
-            pltpu.make_async_copy(landed, landed, recv_sem.at[slot]).wait()
-
-
-def qkv_send(group, heads, normed, cos_t, sin_t, biases, w_q, w_k, w_v):
+
+    def drain_out(slot):
+        def one(dev, carry):
+            @pl.when(dev != me)
+            def _():
+                o_copy(slot, dev).wait_send()
+
+            return carry
+
+        lax.fori_loop(0, group, one, 0)
+        o_local(slot).wait()
+
+    for_slots(drain_out)
+
+    def landed_out(head, carry):
+        @pl.when(owner_of(head, group, heads) != me)
+        def _():
+            back = attn_ref.at[head]
+            pltpu.make_async_copy(back, back, o_recv.at[head]).wait()
+
+        return carry
+
+    lax.fori_loop(0, heads, landed_out, 0)
+
+
+def mixer(group, heads, cu_doc, normed, cos_t, sin_t, biases, w_q, w_k, w_v):
     tokens, width = normed.shape
     slots = -(-heads // group)
+    chips = group // 2
     vmem = pl.BlockSpec(memory_space=pltpu.VMEM)
+    smem = pl.BlockSpec(memory_space=pltpu.SMEM)
     hbm = pl.BlockSpec(memory_space=pl.ANY)
+    state = pltpu.VMEM((slots, chips, 2 * tokens, HEAD_DIM), jnp.float32)
     return pl.pallas_call(
-        functools.partial(qkv_send_kernel, group, heads),
-        out_shape=jax.ShapeDtypeStruct((slots, 3, group, tokens, HEAD_DIM), jnp.bfloat16),
-        in_specs=[vmem, vmem, vmem, vmem, hbm, hbm, hbm],
+        functools.partial(mixer_kernel, group, heads, cu_doc.shape[0] - 2),
+        out_shape=jax.ShapeDtypeStruct((heads, tokens, HEAD_DIM), jnp.bfloat16),
+        in_specs=[smem, vmem, vmem, vmem, vmem, hbm, hbm, hbm],
         out_specs=hbm,
         scratch_shapes=[
             pltpu.VMEM((3, width, 3 * HEAD_DIM), jnp.bfloat16),
             pltpu.VMEM((heads, 3, tokens, HEAD_DIM), jnp.bfloat16),
+            pltpu.VMEM((slots, group, 3, tokens, HEAD_DIM), jnp.bfloat16),
+            state,
+            state,
+            state,
+            pltpu.VMEM((slots, group, tokens, HEAD_DIM), jnp.bfloat16),
             pltpu.SemaphoreType.DMA((3, 3)),
             pltpu.SemaphoreType.DMA((heads,)),
+            pltpu.SemaphoreType.DMA((slots, group)),
             pltpu.SemaphoreType.DMA((slots,)),
+            pltpu.SemaphoreType.DMA((slots, group)),
+            pltpu.SemaphoreType.DMA((heads,)),
             pltpu.SemaphoreType.DMA((slots,)),
         ],
         compiler_params=pltpu.CompilerParams(collective_id=0, has_side_effects=True, vmem_limit_bytes=VMEM_LIMIT),
         cost_estimate=pl.CostEstimate(flops=2 * tokens * width * 3 * heads * HEAD_DIM, bytes_accessed=3 * width * heads * HEAD_DIM * 2, transcendentals=0),
-        name="qkv_send",
-    )(normed, cos_t, sin_t, biases, w_q, w_k, w_v)
-
-
-def attention_kernel(q_rows, k_rows, cuts, info_ref, q_ref, k_ref, v_ref, o_ref):
-    slots = q_ref.shape[0]
-    start = pl.program_id(0) * q_rows
-    low, high = 0, 0
-    for d in range(cuts):
-        low = jnp.where(start >= info_ref[1 + d], info_ref[1 + d], low)
-        high = jnp.where(start + q_rows - 1 >= info_ref[1 + d], info_ref[1 + d], high)
-    q_pos = start + lax.broadcasted_iota(jnp.int32, (q_rows, 1), 0)
-    q_low = jnp.zeros((q_rows, 1), jnp.int32)
-    for d in range(cuts):
-        q_low = jnp.where(q_pos >= info_ref[1 + d], info_ref[1 + d], q_low)
-    scale = HEAD_DIM ** -0.5 * 1.4426950408889634
-    first = low // k_rows
-    diag = start // k_rows
-    inner = jnp.minimum((high + k_rows - 1) // k_rows, diag)
-    last = (start + q_rows - 1) // k_rows
-
-    def run(heads):
-        def step(masked, j, carry):
-            rows = pl.ds(pl.multiple_of(j * k_rows, k_rows), k_rows)
-            if masked:
-                k_pos = j * k_rows + lax.broadcasted_iota(jnp.int32, (1, k_rows), 1)
-                seen = (k_pos <= q_pos) & (k_pos >= q_low)
-            scores, out = [], []
-            for h in range(heads):
-                s = lax.dot_general(q_ref[h], k_ref[h, rows, :], (((1,), (1,)), ((), ())), preferred_element_type=jnp.float32)
-                scores.append(jnp.where(seen, s, -1e30) if masked else s)
-            for h in range(heads):
-                top, total, acc = carry[h]
-                new_top = jnp.maximum(top, jnp.max(scores[h], axis=1, keepdims=True))
-                decay = jnp.exp2((top - new_top) * scale)
-                probs = jnp.exp2((scores[h] - new_top) * scale)
-                total = total * decay + jnp.sum(probs, axis=1, keepdims=True)
-                acc = acc * decay + jnp.dot(probs.astype(jnp.bfloat16), v_ref[h, rows, :], preferred_element_type=jnp.float32)
-                out.append((new_top, total, acc))
-            return tuple(out)
-
-        carry = tuple((jnp.full((q_rows, 1), -1e30, jnp.float32), jnp.zeros((q_rows, 1), jnp.float32), jnp.zeros((q_rows, HEAD_DIM), jnp.float32)) for _ in range(heads))
-        carry = lax.fori_loop(first, inner, functools.partial(step, True), carry)
-        carry = lax.fori_loop(inner, diag, functools.partial(step, False), carry)
-        carry = lax.fori_loop(diag, last + 1, functools.partial(step, True), carry)
-        for h in range(heads):
-            _, total, acc = carry[h]
-            o_ref[h] = (acc / total).astype(jnp.bfloat16)
-
-    for heads in range(1, slots + 1):
-        pl.when(info_ref[0] == heads)(functools.partial(run, heads))
-
-
-def attention(info, qkv, cuts, q_rows, k_rows):
-    slots, _, group, tokens, _ = qkv.shape
-    seq = group * tokens
-    flat = qkv.reshape(slots, 3, seq, HEAD_DIM)
-
-    def whole(part):
-        return pl.BlockSpec((slots, None, seq, HEAD_DIM), lambda i, info: (0, part, 0, 0))
-
-    return pl.pallas_call(
-        functools.partial(attention_kernel, q_rows, k_rows, cuts),
-        grid_spec=pltpu.PrefetchScalarGridSpec(
-            num_scalar_prefetch=1,
-            grid=(seq // q_rows,),
-            in_specs=[pl.BlockSpec((slots, None, q_rows, HEAD_DIM), lambda i, info: (0, 0, i, 0)), whole(1), whole(2)],
-            out_specs=pl.BlockSpec((slots, q_rows, HEAD_DIM), lambda i, info: (0, i, 0)),
-        ),
-        out_shape=jax.ShapeDtypeStruct((slots, seq, HEAD_DIM), jnp.bfloat16),
-        compiler_params=pltpu.CompilerParams(vmem_limit_bytes=VMEM_LIMIT),
-        cost_estimate=pl.CostEstimate(flops=4 * seq * seq * HEAD_DIM, bytes_accessed=8 * seq * HEAD_DIM * slots, transcendentals=seq * seq // 2),
-        name="attention",
-    )(info, flat, flat, flat).reshape(slots, group, tokens, HEAD_DIM)
-
-
-def out_send_kernel(group, heads, o_ref, attn_ref, send_sem, recv_sem, own_sem):
-    me = lax.axis_index("sp")
-    mine = first_head(me, group, heads)
-    count = first_head(me + 1, group, heads) - mine
-    slots = o_ref.shape[0]
-    greet_group(group, me)
-
-    def hop(k):
-        step = k // 2
-        return (me + group // 2 + step - (k % 2) * (2 * step + 1) + group) % group
-
-    def out_copy(slot, k):
-        head = mine + slot
-        return pltpu.make_async_remote_copy(
-            src_ref=o_ref.at[slot, hop(k)],
-            dst_ref=attn_ref.at[head],
-            send_sem=send_sem.at[slot, k],
-            recv_sem=recv_sem.at[head],
-            device_id={"sp": hop(k)},
-            device_id_type=MESH,
-        )
-
-    def own_copy(slot):
-        return pltpu.make_async_copy(o_ref.at[slot, me], attn_ref.at[mine + slot], own_sem.at[slot])
-
-    for slot in range(slots):
-
-        @pl.when(slot < count)
-        def _():
-            for k in range(group - 1):
-                out_copy(slot, k).start()
-            own_copy(slot).start()
-
-    for slot in range(slots):
-
-        @pl.when(slot < count)
-        def _():
-            for k in range(group - 1):
-                out_copy(slot, k).wait_send()
-            own_copy(slot).wait()
-
-    def landed(head, carry):
-        @pl.when(owner_of(head, group, heads) != me)
-        def _():
-            block = attn_ref.at[head]
-            pltpu.make_async_copy(block, block, recv_sem.at[head]).wait()
-
-        return carry
-
-    lax.fori_loop(0, heads, landed, 0)
-
-
-def out_send(group, heads, o_heads):
-    slots, _, tokens, _ = o_heads.shape
-    hbm = pl.BlockSpec(memory_space=pl.ANY)
-    return pl.pallas_call(
-        functools.partial(out_send_kernel, group, heads),
-        out_shape=jax.ShapeDtypeStruct((heads, tokens, HEAD_DIM), jnp.bfloat16),
-        in_specs=[pl.BlockSpec(memory_space=pltpu.VMEM)],
-        out_specs=hbm,
-        scratch_shapes=[
-            pltpu.SemaphoreType.DMA((slots, group - 1)),
-            pltpu.SemaphoreType.DMA((heads,)),
-            pltpu.SemaphoreType.DMA((slots,)),
-        ],
-        compiler_params=pltpu.CompilerParams(collective_id=1, has_side_effects=True),
-        name="out_send",
-    )(o_heads)
+        name="mixer",
+    )(cu_doc, normed, cos_t, sin_t, biases, w_q, w_k, w_v)
 
 
 def place_rows_kernel(group, pieces, merged_ref, slots_ref, embeds_ref, gain_ref, h_ref, a_ref, rows, slots, total, hits, slot_send, slot_recv, ring_send, ring_recv, pair_send, pair_recv):
@@ -527,18 +548,12 @@
         tok_dev = embeds.shape[0]
         merged_dev = dest_slot.shape[0]
         heads = w_q.shape[1] // HEAD_DIM
-        me = lax.axis_index('sp')
         normed = layer_norm(patches, ln_w, ln_b).reshape(merged_dev, -1)
         merged = merger_mlp(normed, w_one, b_one, w_two, b_two)
         h_zero, normed_a = place_rows(group, merged, dest_slot, embeds, norm_attn)
         cos_t, sin_t = rope_tables(rope_pos)
         biases = jnp.concatenate([b.astype(jnp.float32).reshape(heads, 1, HEAD_DIM) for b in (b_q, b_k, b_v)], axis=2)
-        qkv = qkv_send(group, heads, normed_a, cos_t, sin_t, biases, w_q, w_k, w_v)
-        count = first_head(me + 1, group, heads) - first_head(me, group, heads)
-        cuts = cu_doc.shape[0] - 2
-        info = jnp.concatenate([count.astype(jnp.int32).reshape(1), cu_doc[1:-1]])
-        o_heads = attention(info, qkv, cuts, 512, 512)
-        attn_out = out_send(group, heads, o_heads)
+        attn_out = mixer(group, heads, cu_doc, normed_a, cos_t, sin_t, biases, w_q, w_k, w_v)
         return mlp(attn_out, h_zero, norm_mlp, w_o, w_gate, w_up, w_down)
 
     in_specs = (row_spec, row_spec, P(('dp', 'sp')), P(None, ('dp', 'sp')), P('dp')) + (P(),) * 18

time: 338 us -> 292 us (0.86)
  the two profiles are of different devices: /device:TPU:60 before, /device:TPU:21 now
where the time goes in v1:
time: 292 us; the launch traced here: 289 us
  Pallas kernels  252 us (86%)
  matrix products  29.6 us (10%)
  other arithmetic  4.76 us (2%)
  local copies, waits for them, and re-layouts  2.95 us (1%)
    pallas_call x1, Pallas kernels, mixer(): pl.pallas_call(functools.partial(mixer_kernel, group, heads, cu_doc.shape...  139 us
    pallas_call x1, Pallas kernels, place_rows(): pl.pallas_call(functools.partial(place_rows_kernel, group, pieces), out_s...  67.5 us
    pallas_call x1, Pallas kernels, mlp(): pl.pallas_call(functools.partial(mlp_kernel, o_cols, chunk), out_shape=ja...  44.6 us
    dot_general x1, matrix products, merger_mlp(): jnp.dot(inner, w_two, preferred_element_type=jnp.float32)  29.6 us

profile of v1, /device:TPU:21, one launch (start us, length us, event | category | flops | bytes accessed | tf_op | source)
XLA Modules:
  0.0 289.2 jit_solution(14210933375051010696)
XLA Ops:
  0.0 0.0 copy-start
  0.0 0.0 copy-start.8
  0.0 0.8 fusion.82
  0.9 0.6 fusion.51
  1.5 0.8 pad_maximum_fusion
  2.3 1.6 convert_reduce_fusion
  3.9 0.0 copy-done
  3.9 0.5 fusion.3
  4.4 0.0 copy-done.8
  4.4 0.0 copy-done.9
  4.5 0.0 copy-start.1
  4.5 0.0 copy-start.2
  4.5 0.6 fusion.6
  5.0 0.8 reshape.60
  5.9 0.0 copy-done.1
  5.9 0.0 copy-done.2
  5.9 0.0 copy-start.3
  5.9 0.0 copy-start.4
  6.0 0.0 copy-start.5
  6.0 0.0 copy-start.6
  6.0 29.6 %fusion.merged_ref = bf16[128,2560]{1,0:T(8,128)(2,1)} fusion(bf16[5120,2560]{1,0:T(8,128)(2,1)} %param.32, bf16[128,5120]{1,0:T(8,128)(2,1)S(1)} %reshape.60, bf16[5120,5120]{1,0:T(8,128)(2,1)} %param.30, f32[5120]{0:T(1024)S(1)} %convert_element_type.34, f32[2560]{0:T(1024)S(1)} %convert_element_type.36), kind=kOutput, calls=%fused_computation.3 | convolution fusion | flops 10110238720 | bytes 80640000 | tf_op jit(solution)/shard_map/dot_general | solution.py:32
  35.6 0.0 copy-done.3
  35.6 0.6 reshape.62.gain_ref
  36.2 67.5 %place_rows.1 = (bf16[256,2560]{1,0:T(8,128)(2,1)}, bf16[256,2560]{1,0:T(8,128)(2,1)}) custom-call(bf16[128,2560]{1,0:T(8,128)(2,1)} %fusion.merged_ref, s32[1,128]{1,0:T(1,128)} %bitcast.16, bf16[256,2560]{1,0:T(8,128)(2,1)} %embeds_ref.1, bf16[1,2560]{1,0:T(2,128)(2,1)} %reshape.62.gain_ref), custom_call_target="tpu_custom_call" | custom-call | tf_op jit(solution)/shard_map/place_rows/pallas_call | solution.py:435
  103.6 0.0 copy-done.4
  103.7 0.0 copy-done.5
  103.7 0.0 copy-done.6
  103.7 0.6 maximum_convert_fusion.bias_ref
  104.4 139.5 %mixer.1.attn_ref = bf16[20,256,128]{2,1,0:T(8,128)(2,1)} custom-call(s32[5]{0:T(128)} %cu_ref.1, bf16[256,2560]{1,0:T(8,128)(2,1)} %get-tuple-element.7.a_ref, f32[256,128]{1,0:T(8,128)} %get-tuple-element.15.cos_ref, f32[256,128]{1,0:T(8,128)} %get-tuple-element.16.sin_ref, f32[20,1,384]{2,1,0:T(1,128)} %maximum_convert_fusion.bias_ref, ...), custom_call_target="tpu_custom_call" | custom-call | flops 10066329600 | bytes 39321600 | tf_op jit(solution)/shard_map/mixer/pallas_call | solution.py:317
  243.8 0.0 copy-done.7
  243.8 0.6 reshape.66.gain_ref
  244.4 44.6 %mlp.1 = bf16[256,2560]{1,0:T(8,128)(2,1)} custom-call(bf16[20,256,128]{2,1,0:T(8,128)(2,1)} %mixer.1.attn_ref, bf16[256,2560]{1,0:T(8,128)(2,1)} %get-tuple-element.8.h_ref, bf16[1,2560]{1,0:T(2,128)(2,1)} %reshape.66.gain_ref, bf16[2560,2560]{1,0:T(8,128)(2,1)} %wo_ref.1, bf16[2560,6912]{1,0:T(8,128)(2,1)} %wg_ref.1, bf16[2560,6912]{1,0:T(8,128)(2,1)} %wu_ref.1, ...), custom_call_target="tpu_custom_call" | custom-call | flops 30534533120 | bytes 119275520 | tf_op jit(solution)/shard_map/mlp/pallas_call | solution.py:520
  (14 shorter events, 0.1 us)
Async XLA Ops:
  0.0 3.9 %copy-start = (bf16[512,1280]{1,0:T(8,128)(2,1)S(1)}, bf16[512,1280]{1,0:T(8,128)(2,1)}, u32[]{:S(2)}) copy-start(bf16[512,1280]{1,0:T(8,128)(2,1)} %param.23) | copy-start | bytes 3932164
  0.0 4.4 %copy-start.8 = (bf16[1280]{0:T(1024)(128)(2,1)S(1)}, bf16[1280]{0:T(1024)(128)(2,1)}, u32[]{:S(2)}) copy-start(bf16[1280]{0:T(1024)(128)(2,1)} %param.28) | copy-start | bytes 7684
  0.0 4.4 %copy-start.9 = (bf16[1280]{0:T(1024)(128)(2,1)S(1)}, bf16[1280]{0:T(1024)(128)(2,1)}, u32[]{:S(2)}) copy-start(bf16[1280]{0:T(1024)(128)(2,1)} %param.29) | copy-start | bytes 7684
  4.5 1.4 copy-start.1
  4.5 1.4 copy-start.2
  5.9 29.6 %copy-start.3 = (bf16[2560]{0:T(1024)(128)(2,1)S(1)}, bf16[2560]{0:T(1024)(128)(2,1)}, u32[]{:S(2)}) copy-start(bf16[2560]{0:T(1024)(128)(2,1)} %param.34) | copy-start | bytes 15364
  5.9 97.7 %copy-start.4 = (bf16[2560]{0:T(1024)(128)(2,1)S(1)}, bf16[2560]{0:T(1024)(128)(2,1)}, u32[]{:S(2)}) copy-start(bf16[2560]{0:T(1024)(128)(2,1)} %param.36) | copy-start | bytes 15364
  6.0 97.7 %copy-start.5 = (bf16[2560]{0:T(1024)(128)(2,1)S(1)}, bf16[2560]{0:T(1024)(128)(2,1)}, u32[]{:S(2)}) copy-start(bf16[2560]{0:T(1024)(128)(2,1)} %param.38) | copy-start | bytes 15364
  6.0 97.7 %copy-start.6 = (bf16[2560]{0:T(1024)(128)(2,1)S(1)}, bf16[2560]{0:T(1024)(128)(2,1)}, u32[]{:S(2)}) copy-start(bf16[2560]{0:T(1024)(128)(2,1)} %param.40) | copy-start | bytes 15364
  104.4 139.5 %copy-start.7 = (bf16[2560]{0:T(1024)(128)(2,1)S(1)}, bf16[2560]{0:T(1024)(128)(2,1)}, u32[]{:S(2)}) copy-start(bf16[2560]{0:T(1024)(128)(2,1)} %param.42) | copy-start | bytes 15364

commit v2 on v1

--- a/solution.py
+++ b/solution.py
@@ -25,11 +25,6 @@
 def rms_norm(values_in, gain_vec):
     widened = values_in.astype(jnp.float32)
     return (widened * lax.rsqrt(jnp.mean(widened * widened, axis=-1, keepdims=True) + NORM_EPS) * gain_vec.astype(jnp.float32)).astype(jnp.bfloat16)
-
-
-def merger_mlp(grouped, w_one, b_one, w_two, b_two):
-    inner = jax.nn.gelu(jnp.dot(grouped, w_one, preferred_element_type=jnp.float32) + b_one.astype(jnp.float32), approximate=False).astype(jnp.bfloat16)
-    return (jnp.dot(inner, w_two, preferred_element_type=jnp.float32) + b_two.astype(jnp.float32)).astype(jnp.bfloat16)
 
 
 def rope_tables(rope_pos):
@@ -341,18 +336,41 @@
     )(cu_doc, normed, cos_t, sin_t, biases, w_q, w_k, w_v)
 
 
-def place_rows_kernel(group, pieces, merged_ref, slots_ref, embeds_ref, gain_ref, h_ref, a_ref, rows, slots, total, hits, slot_send, slot_recv, ring_send, ring_recv, pair_send, pair_recv):
+def merge_place_kernel(group, patch_ref, lnw_ref, lnb_ref, b1_ref, b2_ref, slots_ref, embeds_ref, gain_ref, w1_ref, w2_ref, h_ref, a_ref, z, wbuf, inner, wide, rows, slots, total, hits, w_sem, z_send, z_recv, in_send, in_recv, slot_send, slot_recv, ring_send, ring_recv, pair_send, pair_recv):
     me = lax.axis_index("sp")
     core = me % 2
-    way = 2 - 4 * core
-    ahead = (me + way + group) % group
+    chip = me // 2
+    chips = group // 2
     other = me + 1 - 2 * core
-    hops = group // 2
-    count = merged_ref.shape[0] // pieces
+    ahead = (me + 2 - 4 * core + group) % group
+    depth = wbuf.shape[0]
+    part = wbuf.shape[2]
+    half_in, half_out = b1_ref.shape[0] // 2, b2_ref.shape[0] // 2
+    count = half_in + half_out
+    merged_dev, merge_dim = patch_ref.shape
+    vit = lnw_ref.shape[1]
+
+    def weight_copy(j):
+        slot = j % depth
+        w_ref, index = (w1_ref, core * half_in + j) if j < half_in else (w2_ref, core * half_out + j - half_in)
+        cols = pl.ds(pl.multiple_of(index * part, part), part)
+        return pltpu.make_async_copy(w_ref.at[:, cols], wbuf.at[slot], w_sem.at[slot])
+
+    for j in range(depth - 1):
+        weight_copy(j).start()
+    for n in range(merge_dim // vit):
+        seg = slice(n * vit, (n + 1) * vit)
+        z[core, :, seg] = layer_norm(patch_ref[:, seg], lnw_ref[...], lnb_ref[...])
+    total[...] = jnp.zeros_like(total)
+    hits[...] = jnp.zeros_like(hits)
+    slots[me] = slots_ref[...]
     greet_group(group, me)
 
-    def origin(dev, step):
-        return (dev - (2 - 4 * (dev % 2)) * step + 2 * group * group) % group
+    def to_other(src, dst, send_sem, recv_sem):
+        return pltpu.make_async_remote_copy(src_ref=src, dst_ref=dst, send_sem=send_sem, recv_sem=recv_sem, device_id={"sp": other}, device_id_type=MESH)
+
+    def arrive(ref, sem):
+        pltpu.make_async_copy(ref, ref, sem).wait()
 
     def slot_copy(k):
         return pltpu.make_async_remote_copy(
@@ -360,98 +378,159 @@
             device_id={"sp": lax.rem(me + k, group)}, device_id_type=MESH,
         )
 
-    def block(ref, step, piece):
-        return ref.at[origin(me, step), pl.ds(piece * count, count)]
-
-    def source(step, piece):
-        return merged_ref.at[pl.ds(piece * count, count)] if step == 0 else block(rows, step, piece)
-
-    def ring_copy(step, piece):
-        return pltpu.make_async_remote_copy(
-            src_ref=source(step, piece), dst_ref=block(rows, step, piece), send_sem=ring_send.at[step, piece],
-            recv_sem=ring_recv.at[step, piece], device_id={"sp": ahead}, device_id_type=MESH,
-        )
-
-    def pair_copy(step, piece):
-        return pltpu.make_async_remote_copy(
-            src_ref=source(step, piece), dst_ref=block(rows, step, piece), send_sem=pair_send.at[step, piece],
-            recv_sem=pair_recv.at[step, piece], device_id={"sp": other}, device_id_type=MESH,
-        )
-
+    z_copy = to_other(z.at[core], z.at[core], z_send, z_recv)
+    z_copy.start()
     for k in range(1, group):
         slot_copy(k).start()
-    for piece in range(pieces):
-        ring_copy(0, piece).start()
-        pair_copy(0, piece).start()
-    slots[me] = slots_ref[...]
-    total[...] = jnp.zeros_like(total)
-    hits[...] = jnp.zeros_like(hits)
+    arrive(z.at[1 - core], z_recv)
+
+    def inner_copy(j):
+        mine = inner.at[core * half_in + j]
+        return to_other(mine, mine, in_send.at[j], in_recv.at[j])
+
+    def origin(lane, step):
+        return (chip - (1 - 2 * lane) * step + chips) % chips
+
+    def ring_copy(step, piece):
+        held = rows.at[core, origin(core, step), piece]
+        return pltpu.make_async_remote_copy(
+            src_ref=held, dst_ref=held, send_sem=ring_send.at[step, piece], recv_sem=ring_recv.at[step, piece],
+            device_id={"sp": ahead}, device_id_type=MESH,
+        )
+
+    def pair_copy(step, piece):
+        held = rows.at[core, origin(core, step), piece]
+        return to_other(held, held, pair_send.at[step, piece], pair_recv.at[step, piece])
+
+    for j in range(half_in):
+        weight_copy(j + depth - 1).start()
+        weight_copy(j).wait()
+        lin = jnp.dot(z[...].reshape(2 * merged_dev, merge_dim), wbuf[j % depth], preferred_element_type=jnp.float32)
+        lin = lin + b1_ref[core * half_in + j].astype(jnp.float32)
+        inner[core * half_in + j] = (lin * (0.5 * (1.0 + lax.erf(lin * 0.7071067811865476)))).astype(jnp.bfloat16)
+        if j > 0:
+            inner_copy(j - 1).start()
+    inner_copy(half_in - 1).start()
+    for j in range(half_in):
+        arrive(inner.at[(1 - core) * half_in + j], in_recv.at[j])
+    for j in range(2 * half_in):
+        wide[:, j * part:(j + 1) * part] = inner[j]
+    for j in range(half_in, count):
+        piece = j - half_in
+        if j + depth - 1 < count:
+            weight_copy(j + depth - 1).start()
+        weight_copy(j).wait()
+        lin = jnp.dot(wide[...], wbuf[j % depth], preferred_element_type=jnp.float32)
+        rows[core, chip, piece] = (lin + b2_ref[core * half_out + piece].astype(jnp.float32)).astype(jnp.bfloat16)
+        if piece > 0:
+            ring_copy(0, piece - 1).start()
+            pair_copy(0, piece - 1).start()
     tokens = embeds_ref.shape[0]
-
-    def place(dev, values):
-        wanted = me * tokens + lax.broadcasted_iota(jnp.int32, (tokens, 1), 0)
-        pick = jnp.where(slots[dev] == wanted, 1.0, 0.0)
-        hits[...] += pick
-        total[...] += jnp.dot(pick.astype(jnp.bfloat16), values, preferred_element_type=jnp.float32)
-
+    wanted = me * tokens + lax.broadcasted_iota(jnp.int32, (tokens, 1), 0)
     for k in range(1, group):
         dev = lax.rem(me + k, group)
-        pltpu.make_async_copy(slots.at[dev], slots.at[dev], slot_recv.at[dev]).wait()
-    place(me, merged_ref[...])
-    for step in range(hops):
-        if step > 0:
-            for piece in range(pieces):
-                landed = block(rows, step, piece)
-                pltpu.make_async_copy(landed, landed, ring_recv.at[step - 1, piece]).wait()
-                if step < hops - 1:
+        arrive(slots.at[dev], slot_recv.at[dev])
+    ring_copy(0, half_out - 1).start()
+    pair_copy(0, half_out - 1).start()
+
+    def choose(block):
+        return jnp.concatenate([jnp.where(slots[2 * block + n] == wanted, 1.0, 0.0) for n in range(2)], axis=1)
+
+    def place(lane, block, pick):
+        for piece in range(half_out):
+            total[lane * half_out + piece] += jnp.dot(pick, rows[lane, block, piece], preferred_element_type=jnp.float32)
+
+    def hop(step, carry):
+        mine, theirs = origin(core, step), origin(1 - core, step)
+
+        @pl.when(step > 0)
+        def _():
+            for piece in range(half_out):
+                arrive(rows.at[core, mine, piece], ring_recv.at[(step + chips - 1) % chips, piece])
+
+                @pl.when(step < chips - 1)
+                def _():
                     ring_copy(step, piece).start()
+
                 pair_copy(step, piece).start()
-            place(origin(me, step), rows[origin(me, step)])
-        theirs = origin(other, step)
-        for piece in range(pieces):
-            landed = rows.at[theirs, pl.ds(piece * count, count)]
-            pltpu.make_async_copy(landed, landed, pair_recv.at[step, piece]).wait()
-        place(theirs, rows[theirs])
+
+        pick = choose(mine)
+        hits[...] += pick
+        place(core, mine, pick.astype(jnp.bfloat16))
+        for piece in range(half_out):
+            arrive(rows.at[1 - core, theirs, piece], pair_recv.at[step, piece])
+        place(1 - core, theirs, choose(theirs).astype(jnp.bfloat16))
+        return carry
+
+    lax.fori_loop(0, chips, hop, 0)
     found = jnp.max(hits[...], axis=1, keepdims=True) > 0.0
-    h_zero = jnp.where(found, total[...].astype(jnp.bfloat16), embeds_ref[...])
-    h_ref[...] = h_zero
-    a_ref[...] = rms_norm(h_zero, gain_ref[...])
+    for n in range(2 * half_out):
+        cols = slice(n * part, (n + 1) * part)
+        h_ref[:, cols] = jnp.where(found, total[n].astype(jnp.bfloat16), embeds_ref[:, cols])
+    a_ref[...] = rms_norm(h_ref[...], gain_ref[...])
+    z_copy.wait_send()
     for k in range(1, group):
         slot_copy(k).wait_send()
-    for step in range(hops):
-        for piece in range(pieces):
-            if step < hops - 1:
+    for j in range(half_in):
+        inner_copy(j).wait_send()
+
+    def drain(step, carry):
+        for piece in range(half_out):
+            @pl.when(step < chips - 1)
+            def _():
                 ring_copy(step, piece).wait_send()
+
             pair_copy(step, piece).wait_send()
-
-
-def place_rows(group, merged, dest_slot, embeds, gain):
-    rows, width = merged.shape
+        return carry
+
+    lax.fori_loop(0, chips, drain, 0)
+
+
+def merge_place(group, patches, ln_w, ln_b, w_one, b_one, w_two, b_two, dest_slot, embeds, gain):
+    merged_dev = dest_slot.shape[0]
+    merge_dim, width = w_two.shape
     tokens = embeds.shape[0]
-    pieces = 4
-    hops = group // 2
+    vit = ln_w.shape[0]
+    part = 2 * HEAD_DIM
+    chips = group // 2
+    n_in, n_out = merge_dim // part, width // part
     vmem = pl.BlockSpec(memory_space=pltpu.VMEM)
+    hbm = pl.BlockSpec(memory_space=pl.ANY)
     out = jax.ShapeDtypeStruct((tokens, width), jnp.bfloat16)
+    ring = pltpu.SemaphoreType.DMA((chips, n_out // 2))
     return pl.pallas_call(
-        functools.partial(place_rows_kernel, group, pieces),
+        functools.partial(merge_place_kernel, group),
         out_shape=(out, out),
-        in_specs=[vmem] * 4,
+        in_specs=[vmem] * 8 + [hbm, hbm],
         out_specs=(vmem, vmem),
         scratch_shapes=[
-            pltpu.VMEM((group, rows, width), jnp.bfloat16),
-            pltpu.VMEM((group, 1, rows), jnp.int32),
-            pltpu.VMEM((tokens, width), jnp.float32),
-            pltpu.VMEM((tokens, rows), jnp.float32),
+            pltpu.VMEM((2, merged_dev, merge_dim), jnp.bfloat16),
+            pltpu.VMEM((3, merge_dim, part), jnp.bfloat16),
+            pltpu.VMEM((n_in, 2 * merged_dev, part), jnp.bfloat16),
+            pltpu.VMEM((2 * merged_dev, merge_dim), jnp.bfloat16),
+            pltpu.VMEM((2, chips, n_out // 2, 2 * merged_dev, part), jnp.bfloat16),
+            pltpu.VMEM((group, 1, merged_dev), jnp.int32),
+            pltpu.VMEM((n_out, tokens, part), jnp.float32),
+            pltpu.VMEM((tokens, 2 * merged_dev), jnp.float32),
+            pltpu.SemaphoreType.DMA((3,)),
+            pltpu.SemaphoreType.DMA,
+            pltpu.SemaphoreType.DMA,
+            pltpu.SemaphoreType.DMA((n_in // 2,)),
+            pltpu.SemaphoreType.DMA((n_in // 2,)),
             pltpu.SemaphoreType.DMA((group,)),
             pltpu.SemaphoreType.DMA((group,)),
-            pltpu.SemaphoreType.DMA((hops, pieces)),
-            pltpu.SemaphoreType.DMA((hops, pieces)),
-            pltpu.SemaphoreType.DMA((hops, pieces)),
-            pltpu.SemaphoreType.DMA((hops, pieces)),
+            ring,
+            ring,
+            ring,
+            ring,
         ],
         compiler_params=pltpu.CompilerParams(collective_id=2, has_side_effects=True, vmem_limit_bytes=VMEM_LIMIT),
-        name="place_rows",
-    )(merged, dest_slot.reshape(1, rows), embeds, gain.reshape(1, width))
+        cost_estimate=pl.CostEstimate(flops=2 * merged_dev * merge_dim * (merge_dim + width), bytes_accessed=merge_dim * (merge_dim + width), transcendentals=0),
+        name="merge_place",
+    )(
+        patches.reshape(merged_dev, merge_dim), ln_w.reshape(1, vit), ln_b.reshape(1, vit), b_one.reshape(n_in, 1, part), b_two.reshape(n_out, 1, part),
+        dest_slot.reshape(1, merged_dev), embeds, gain.reshape(1, width), w_one, w_two,
+    )
 
 
 def mlp_kernel(o_cols, chunk, attn_ref, h_ref, gain_ref, wo_ref, wg_ref, wu_ref, wd_ref, out_ref, attn, h_one, normed, total, wo, wg, wu, wd, o_sem, f_sem):
@@ -545,12 +624,8 @@
     row_spec = P(('dp', 'sp'), None)
 
     def local_step(patches, embeds, dest_slot, rope_pos, cu_doc, ln_w, ln_b, w_one, b_one, w_two, b_two, norm_attn, w_q, b_q, w_k, b_k, w_v, b_v, w_o, norm_mlp, w_gate, w_up, w_down):
-        tok_dev = embeds.shape[0]
-        merged_dev = dest_slot.shape[0]
         heads = w_q.shape[1] // HEAD_DIM
-        normed = layer_norm(patches, ln_w, ln_b).reshape(merged_dev, -1)
-        merged = merger_mlp(normed, w_one, b_one, w_two, b_two)
-        h_zero, normed_a = place_rows(group, merged, dest_slot, embeds, norm_attn)
+        h_zero, normed_a = merge_place(group, patches, ln_w, ln_b, w_one, b_one, w_two, b_two, dest_slot, embeds, norm_attn)
         cos_t, sin_t = rope_tables(rope_pos)
         biases = jnp.concatenate([b.astype(jnp.float32).reshape(heads, 1, HEAD_DIM) for b in (b_q, b_k, b_v)], axis=2)
         attn_out = mixer(group, heads, cu_doc, normed_a, cos_t, sin_t, biases, w_q, w_k, w_v)

time: 292 us -> 291 us (level)
  matrix products: 29.6 us -> 0 us
  Pallas kernels: 252 us -> 276 us
  local copies, waits for them, and re-layouts: 2.95 us -> 10.4 us
    dot_general x1 -> x0, matrix products: 29.6 us -> none  [merger_mlp(): jnp.dot(inner, w_two, preferred_element_type=jnp.float32)]
    pallas_call x1, Pallas kernels: 67.5 us -> 91.8 us  [merge_place(): pl.pallas_call(functools.partial(merge_place_kernel, group), out_shape=(o...]
    reshape x2 -> x6, local copies, waits for them, and re-layouts: 1.44 us -> 9.78 us  [the longest x1 3.31 us: merge_place(): patches.reshape(merged_dev, merge_dim)]
where the time goes in v2:
time: 291 us; the launch traced here: 289 us
  Pallas kernels  276 us (95%)
  local copies, waits for them, and re-layouts  10.4 us (4%)
    pallas_call x1, Pallas kernels, mixer(): pl.pallas_call(functools.partial(mixer_kernel, group, heads, cu_doc.shape...  140 us
    pallas_call x1, Pallas kernels, merge_place(): pl.pallas_call(functools.partial(merge_place_kernel, group), out_shape=(o...  91.8 us
    pallas_call x1, Pallas kernels, mlp(): pl.pallas_call(functools.partial(mlp_kernel, o_cols, chunk), out_shape=ja...  44.6 us

profile of v2, /device:TPU:21, one launch (start us, length us, event | category | flops | bytes accessed | tf_op | source)
XLA Modules:
  0.0 289.1 jit_solution(4454700427416530834)
XLA Ops:
  0.0 3.3 %reshape.56.patch_ref = bf16[128,5120]{1,0:T(8,128)(2,1)} reshape(bf16[512,1280]{1,0:T(8,128)(2,1)} %param.23) | data formatting | bytes 2621440 | tf_op jit(solution)/shard_map/reshape | solution.py:531
  3.3 1.3 reshape.57.lnw_ref
  4.6 1.3 reshape.58.lnb_ref
  5.9 1.3 reshape.67.b1_ref
  7.2 1.3 reshape.68.b2_ref
  8.5 1.3 reshape.62.gain_ref
  9.8 0.0 copy-start.4
  9.8 0.0 copy-start
  9.8 0.0 copy-start.1
  9.8 0.0 copy-start.2
  9.8 91.8 %merge_place.1 = (bf16[256,2560]{1,0:T(8,128)(2,1)}, bf16[256,2560]{1,0:T(8,128)(2,1)}) custom-call(bf16[128,5120]{1,0:T(8,128)(2,1)} %reshape.56.patch_ref, bf16[1,1280]{1,0:T(2,128)(2,1)} %reshape.57.lnw_ref, bf16[1,1280]{1,0:T(2,128)(2,1)} %reshape.58.lnb_ref, bf16[20,1,256]{2,1,0:T(2,128)(2,1)} %reshape.67.b1_ref, bf16[10,1,256]{2,1,0:T(2,128)(2,1)} %reshape.68.b2_ref, ...), custom_call_target="tpu_custom_call" | custom-call | flops 10066329600 | bytes 39321600 | tf_op jit(solution)/shard_map/merge_place/pallas_call | solution.py:501
  101.6 0.0 copy-done.4
  101.7 0.6 fusion.2
  102.3 0.8 pad_maximum_fusion
  103.1 0.0 copy-done
  103.2 0.0 copy-done.1
  103.2 0.0 copy-done.2
  103.2 0.7 maximum_convert_fusion.bias_ref
  103.9 0.0 copy-start.3
  103.9 139.8 %mixer.1.attn_ref = bf16[20,256,128]{2,1,0:T(8,128)(2,1)} custom-call(s32[5]{0:T(128)} %cu_ref.1, bf16[256,2560]{1,0:T(8,128)(2,1)} %get-tuple-element.7.a_ref, f32[256,128]{1,0:T(8,128)} %get-tuple-element.15.cos_ref, f32[256,128]{1,0:T(8,128)} %get-tuple-element.16.sin_ref, f32[20,1,384]{2,1,0:T(1,128)} %maximum_convert_fusion.bias_ref, ...), custom_call_target="tpu_custom_call" | custom-call | flops 10066329600 | bytes 39321600 | tf_op jit(solution)/shard_map/mixer/pallas_call | solution.py:312
  243.7 0.0 copy-done.3
  243.7 0.6 reshape.66.gain_ref
  244.3 44.6 %mlp.1 = bf16[256,2560]{1,0:T(8,128)(2,1)} custom-call(bf16[20,256,128]{2,1,0:T(8,128)(2,1)} %mixer.1.attn_ref, bf16[256,2560]{1,0:T(8,128)(2,1)} %get-tuple-element.8.h_ref, bf16[1,2560]{1,0:T(2,128)(2,1)} %reshape.66.gain_ref, bf16[2560,2560]{1,0:T(8,128)(2,1)} %wo_ref.1, bf16[2560,6912]{1,0:T(8,128)(2,1)} %wg_ref.1, bf16[2560,6912]{1,0:T(8,128)(2,1)} %wu_ref.1, ...), custom_call_target="tpu_custom_call" | custom-call | flops 30534533120 | bytes 119275520 | tf_op jit(solution)/shard_map/mlp/pallas_call | solution.py:599
  (7 shorter events, 0.1 us)
Async XLA Ops:
  9.8 91.8 %copy-start.4 = (s32[3,256]{1,0:T(4,128)S(1)}, s32[3,256]{1,0:T(4,128)}, u32[]{:S(2)}) copy-start(s32[3,256]{1,0:T(4,128)} %param.26) | copy-start | bytes 9220
  9.8 93.4 %copy-start = (bf16[2560]{0:T(1024)(128)(2,1)S(1)}, bf16[2560]{0:T(1024)(128)(2,1)}, u32[]{:S(2)}) copy-start(bf16[2560]{0:T(1024)(128)(2,1)} %param.40) | copy-start | bytes 15364
  9.8 93.4 %copy-start.1 = (bf16[2560]{0:T(1024)(128)(2,1)S(1)}, bf16[2560]{0:T(1024)(128)(2,1)}, u32[]{:S(2)}) copy-start(bf16[2560]{0:T(1024)(128)(2,1)} %param.38) | copy-start | bytes 15364
  9.8 93.4 %copy-start.2 = (bf16[2560]{0:T(1024)(128)(2,1)S(1)}, bf16[2560]{0:T(1024)(128)(2,1)}, u32[]{:S(2)}) copy-start(bf16[2560]{0:T(1024)(128)(2,1)} %param.36) | copy-start | bytes 15364
  103.9 139.8 %copy-start.3 = (bf16[2560]{0:T(1024)(128)(2,1)S(1)}, bf16[2560]{0:T(1024)(128)(2,1)}, u32[]{:S(2)}) copy-start(bf16[2560]{0:T(1024)(128)(2,1)} %param.42) | copy-start | bytes 15364

commit v3 on v2

--- a/solution.py
+++ b/solution.py
@@ -13,13 +13,8 @@
 MROPE_SPLIT = (16, 40)
 MESH = pl.DeviceIdType.MESH
 VMEM_LIMIT = 60 * 1024 * 1024
-
-
-def layer_norm(values_in, gain_vec, shift_vec):
-    widened = values_in.astype(jnp.float32)
-    centered = widened - jnp.mean(widened, axis=-1, keepdims=True)
-    spread = jnp.mean(centered * centered, axis=-1, keepdims=True)
-    return (centered * lax.rsqrt(spread + NORM_EPS) * gain_vec.astype(jnp.float32) + shift_vec.astype(jnp.float32)).astype(jnp.bfloat16)
+MIXER_VMEM = 42 * 1024 * 1024
+MLP_VMEM = 46 * 1024 * 1024
 
 
 def rms_norm(values_in, gain_vec):
@@ -51,7 +46,7 @@
     pl.semaphore_wait(barrier, group - 1)
 
 
-def mixer_kernel(group, heads, cuts, cu_ref, a_ref, cos_ref, sin_ref, bias_ref, wq_ref, wk_ref, wv_ref, attn_ref, wbuf, stage, land, top_ref, sum_ref, acc_ref, o_ref, w_sem, send_sem, recv_sem, own_sem, o_send, o_recv, o_own):
+def mixer_kernel(group, heads, cuts, bias_at, cu_ref, a_ref, cos_ref, sin_ref, vec_ref, wq_ref, wk_ref, wv_ref, attn_ref, wbuf, stage, land, top_ref, sum_ref, acc_ref, o_ref, w_sem, send_sem, recv_sem, own_sem, o_send, o_recv, o_own):
     me = lax.axis_index("sp")
     chips = group // 2
     my_chip = me // 2
@@ -113,7 +108,8 @@
 
         for c in weight_copies(p):
             c.wait()
-        lin = jnp.dot(a_ref[...], wbuf[p % depth], preferred_element_type=jnp.float32) + bias_ref[head_at(p)]
+        lin = jnp.dot(a_ref[...], wbuf[p % depth], preferred_element_type=jnp.float32)
+        lin = lin + jnp.concatenate([vec_ref[:, pl.ds(pl.multiple_of(at + head_at(p) * HEAD_DIM, HEAD_DIM), HEAD_DIM)] for at in bias_at], axis=1)
 
         @pl.when(p > 0)
         def _():
@@ -301,7 +297,7 @@
     lax.fori_loop(0, heads, landed_out, 0)
 
 
-def mixer(group, heads, cu_doc, normed, cos_t, sin_t, biases, w_q, w_k, w_v):
+def mixer(group, heads, cu_doc, normed, cos_t, sin_t, vectors, bias_at, w_q, w_k, w_v):
     tokens, width = normed.shape
     slots = -(-heads // group)
     chips = group // 2
@@ -310,7 +306,7 @@
     hbm = pl.BlockSpec(memory_space=pl.ANY)
     state = pltpu.VMEM((slots, chips, 2 * tokens, HEAD_DIM), jnp.float32)
     return pl.pallas_call(
-        functools.partial(mixer_kernel, group, heads, cu_doc.shape[0] - 2),
+        functools.partial(mixer_kernel, group, heads, cu_doc.shape[0] - 2, bias_at),
         out_shape=jax.ShapeDtypeStruct((heads, tokens, HEAD_DIM), jnp.bfloat16),
         in_specs=[smem, vmem, vmem, vmem, vmem, hbm, hbm, hbm],
         out_specs=hbm,
@@ -330,13 +326,13 @@
             pltpu.SemaphoreType.DMA((heads,)),
             pltpu.SemaphoreType.DMA((slots,)),
         ],
-        compiler_params=pltpu.CompilerParams(collective_id=0, has_side_effects=True, vmem_limit_bytes=VMEM_LIMIT),
+        compiler_params=pltpu.CompilerParams(collective_id=0, has_side_effects=True, vmem_limit_bytes=MIXER_VMEM),
         cost_estimate=pl.CostEstimate(flops=2 * tokens * width * 3 * heads * HEAD_DIM, bytes_accessed=3 * width * heads * HEAD_DIM * 2, transcendentals=0),
         name="mixer",
-    )(cu_doc, normed, cos_t, sin_t, biases, w_q, w_k, w_v)
-
-
-def merge_place_kernel(group, patch_ref, lnw_ref, lnb_ref, b1_ref, b2_ref, slots_ref, embeds_ref, gain_ref, w1_ref, w2_ref, h_ref, a_ref, z, wbuf, inner, wide, rows, slots, total, hits, w_sem, z_send, z_recv, in_send, in_recv, slot_send, slot_recv, ring_send, ring_recv, pair_send, pair_recv):
+    )(cu_doc, normed, cos_t, sin_t, vectors, w_q, w_k, w_v)
+
+
+def merge_place_kernel(group, patch_ref, vec_ref, slots_ref, embeds_ref, w1_ref, w2_ref, h_ref, a_ref, z, scaled, wbuf, inner, wide, rows, slots, total, hits, w_sem, z_send, z_recv, in_send, in_recv, slot_send, slot_recv, ring_send, ring_recv, pair_send, pair_recv):
     me = lax.axis_index("sp")
     core = me % 2
     chip = me // 2
@@ -345,10 +341,19 @@
     ahead = (me + 2 - 4 * core + group) % group
     depth = wbuf.shape[0]
     part = wbuf.shape[2]
-    half_in, half_out = b1_ref.shape[0] // 2, b2_ref.shape[0] // 2
+    merged_dev, vit = slots_ref.shape[1], patch_ref.shape[1]
+    merge_dim, width = w2_ref.shape
+    half_in, half_out = merge_dim // (2 * part), width // (2 * part)
     count = half_in + half_out
-    merged_dev, merge_dim = patch_ref.shape
-    vit = lnw_ref.shape[1]
+    after = [0]
+    for size in (vit, vit, merge_dim, width, width):
+        after.append(after[-1] + size)
+
+    def vector(n):
+        return vec_ref[:, after[n]:after[n + 1]]
+
+    def bias(n, index):
+        return vec_ref[:, pl.ds(pl.multiple_of(after[n] + index * part, HEAD_DIM), part)]
 
     def weight_copy(j):
         slot = j % depth
@@ -358,9 +363,17 @@
 
     for j in range(depth - 1):
         weight_copy(j).start()
-    for n in range(merge_dim // vit):
-        seg = slice(n * vit, (n + 1) * vit)
-        z[core, :, seg] = layer_norm(patch_ref[:, seg], lnw_ref[...], lnb_ref[...])
+    widened = patch_ref[...].astype(jnp.float32)
+    centered = widened - jnp.mean(widened, axis=-1, keepdims=True)
+    spread = jnp.mean(centered * centered, axis=-1, keepdims=True)
+    normed = centered * lax.rsqrt(spread + NORM_EPS) * vector(0) + vector(1)
+    for c in range(vit // HEAD_DIM):
+        scaled[c] = normed[:, c * HEAD_DIM:(c + 1) * HEAD_DIM]
+    merge = merge_dim // vit
+    for n in range(merge):
+        for c in range(vit // HEAD_DIM):
+            lanes = n * vit + c * HEAD_DIM
+            z[core, :, lanes:lanes + HEAD_DIM] = scaled[c, pl.ds(n, merged_dev, stride=merge), :].astype(jnp.bfloat16)
     total[...] = jnp.zeros_like(total)
     hits[...] = jnp.zeros_like(hits)
     slots[me] = slots_ref[...]
@@ -406,7 +419,7 @@
         weight_copy(j + depth - 1).start()
         weight_copy(j).wait()
         lin = jnp.dot(z[...].reshape(2 * merged_dev, merge_dim), wbuf[j % depth], preferred_element_type=jnp.float32)
-        lin = lin + b1_ref[core * half_in + j].astype(jnp.float32)
+        lin = lin + bias(2, core * half_in + j)
         inner[core * half_in + j] = (lin * (0.5 * (1.0 + lax.erf(lin * 0.7071067811865476)))).astype(jnp.bfloat16)
         if j > 0:
             inner_copy(j - 1).start()
@@ -421,7 +434,7 @@
             weight_copy(j + depth - 1).start()
         weight_copy(j).wait()
         lin = jnp.dot(wide[...], wbuf[j % depth], preferred_element_type=jnp.float32)
-        rows[core, chip, piece] = (lin + b2_ref[core * half_out + piece].astype(jnp.float32)).astype(jnp.bfloat16)
+        rows[core, chip, piece] = (lin + bias(3, core * half_out + piece)).astype(jnp.bfloat16)
         if piece > 0:
             ring_copy(0, piece - 1).start()
             pair_copy(0, piece - 1).start()
@@ -436,17 +449,19 @@
     def choose(block):
         return jnp.concatenate([jnp.where(slots[2 * block + n] == wanted, 1.0, 0.0) for n in range(2)], axis=1)
 
-    def place(lane, block, pick):
+    def place(lane, block, piece, pick):
+        total[lane * half_out + piece] += jnp.dot(pick, rows[lane, block, piece], preferred_element_type=jnp.float32)
+
+    def hop(step, carry):
+        mine, theirs = origin(core, step - 1), origin(1 - core, step - 1)
+        pick, pick_theirs = choose(mine), choose(theirs).astype(jnp.bfloat16)
+        hits[...] += pick
+        pick = pick.astype(jnp.bfloat16)
         for piece in range(half_out):
-            total[lane * half_out + piece] += jnp.dot(pick, rows[lane, block, piece], preferred_element_type=jnp.float32)
-
-    def hop(step, carry):
-        mine, theirs = origin(core, step), origin(1 - core, step)
-
-        @pl.when(step > 0)
-        def _():
-            for piece in range(half_out):
-                arrive(rows.at[core, mine, piece], ring_recv.at[(step + chips - 1) % chips, piece])
+
+            @pl.when(step < chips)
+            def _():
+                arrive(rows.at[core, origin(core, step), piece], ring_recv.at[step - 1, piece])
 
                 @pl.when(step < chips - 1)
                 def _():
@@ -454,20 +469,17 @@
 
                 pair_copy(step, piece).start()
 
-        pick = choose(mine)
-        hits[...] += pick
-        place(core, mine, pick.astype(jnp.bfloat16))
-        for piece in range(half_out):
-            arrive(rows.at[1 - core, theirs, piece], pair_recv.at[step, piece])
-        place(1 - core, theirs, choose(theirs).astype(jnp.bfloat16))
-        return carry
-
-    lax.fori_loop(0, chips, hop, 0)
+            place(core, mine, piece, pick)
+            arrive(rows.at[1 - core, theirs, piece], pair_recv.at[step - 1, piece])
+            place(1 - core, theirs, piece, pick_theirs)
+        return carry
+
+    lax.fori_loop(1, chips + 1, hop, 0)
     found = jnp.max(hits[...], axis=1, keepdims=True) > 0.0
     for n in range(2 * half_out):
         cols = slice(n * part, (n + 1) * part)
         h_ref[:, cols] = jnp.where(found, total[n].astype(jnp.bfloat16), embeds_ref[:, cols])
-    a_ref[...] = rms_norm(h_ref[...], gain_ref[...])
+    a_ref[...] = rms_norm(h_ref[...], vector(4))
     z_copy.wait_send()
     for k in range(1, group):
         slot_copy(k).wait_send()
@@ -486,11 +498,10 @@
     lax.fori_loop(0, chips, drain, 0)
 
 
-def merge_place(group, patches, ln_w, ln_b, w_one, b_one, w_two, b_two, dest_slot, embeds, gain):
+def merge_place(group, patches, vectors, w_one, w_two, dest_slot, embeds):
     merged_dev = dest_slot.shape[0]
     merge_dim, width = w_two.shape
     tokens = embeds.shape[0]
-    vit = ln_w.shape[0]
     part = 2 * HEAD_DIM
     chips = group // 2
     n_in, n_out = merge_dim // part, width // part
@@ -501,10 +512,11 @@
     return pl.pallas_call(
         functools.partial(merge_place_kernel, group),
         out_shape=(out, out),
-        in_specs=[vmem] * 8 + [hbm, hbm],
+        in_specs=[vmem] * 4 + [hbm, hbm],
         out_specs=(vmem, vmem),
         scratch_shapes=[
             pltpu.VMEM((2, merged_dev, merge_dim), jnp.bfloat16),
+            pltpu.VMEM((patches.shape[1] // HEAD_DIM, patches.shape[0], HEAD_DIM), jnp.float32),
             pltpu.VMEM((3, merge_dim, part), jnp.bfloat16),
             pltpu.VMEM((n_in, 2 * merged_dev, part), jnp.bfloat16),
             pltpu.VMEM((2 * merged_dev, merge_dim), jnp.bfloat16),
@@ -528,12 +540,12 @@
         cost_estimate=pl.CostEstimate(flops=2 * merged_dev * merge_dim * (merge_dim + width), bytes_accessed=merge_dim * (merge_dim + width), transcendentals=0),
         name="merge_place",
     )(
-        patches.reshape(merged_dev, merge_dim), ln_w.reshape(1, vit), ln_b.reshape(1, vit), b_one.reshape(n_in, 1, part), b_two.reshape(n_out, 1, part),
-        dest_slot.reshape(1, merged_dev), embeds, gain.reshape(1, width), w_one, w_two,
+        patches, vectors,
+        dest_slot.reshape(1, merged_dev), embeds, w_one, w_two,
     )
 
 
-def mlp_kernel(o_cols, chunk, attn_ref, h_ref, gain_ref, wo_ref, wg_ref, wu_ref, wd_ref, out_ref, attn, h_one, normed, total, wo, wg, wu, wd, o_sem, f_sem):
+def mlp_kernel(o_cols, chunk, gain_at, attn_ref, h_ref, vec_ref, wo_ref, wg_ref, wu_ref, wd_ref, out_ref, attn, h_one, normed, total, wo, wg, wu, wd, o_sem, f_sem):
     heads, _, dim = attn_ref.shape
     width = h_ref.shape[1]
     o_steps, steps = width // o_cols, wg_ref.shape[1] // chunk
@@ -564,7 +576,7 @@
         if i == o_steps - 3:
             for c in f_copies(0):
                 c.start()
-    normed[...] = rms_norm(h_one[...], gain_ref[...])
+    normed[...] = rms_norm(h_one[...], vec_ref[:, gain_at:gain_at + width])
     total[...] = h_one[...].astype(jnp.float32)
 
     def step(i, carry):
@@ -589,7 +601,7 @@
     out_ref[...] = total[...].astype(jnp.bfloat16)
 
 
-def mlp(attn, h_zero, gain, w_o, w_gate, w_up, w_down):
+def mlp(attn, h_zero, vectors, gain_at, w_o, w_gate, w_up, w_down):
     heads, tokens, dim = attn.shape
     width, ffn = w_gate.shape
     o_cols = width // 5
@@ -597,7 +609,7 @@
     vmem = pl.BlockSpec(memory_space=pltpu.VMEM)
     hbm = pl.BlockSpec(memory_space=pl.ANY)
     return pl.pallas_call(
-        functools.partial(mlp_kernel, o_cols, chunk),
+        functools.partial(mlp_kernel, o_cols, chunk, gain_at),
         out_shape=jax.ShapeDtypeStruct((tokens, width), jnp.bfloat16),
         in_specs=[vmem, vmem, vmem, hbm, hbm, hbm, hbm],
         out_specs=vmem,
@@ -613,10 +625,10 @@
             pltpu.SemaphoreType.DMA((2,)),
             pltpu.SemaphoreType.DMA((2, 3)),
         ],
-        compiler_params=pltpu.CompilerParams(vmem_limit_bytes=VMEM_LIMIT),
+        compiler_params=pltpu.CompilerParams(vmem_limit_bytes=MLP_VMEM),
         cost_estimate=pl.CostEstimate(flops=2 * tokens * width * (3 * ffn + width), bytes_accessed=2 * width * (3 * ffn + width), transcendentals=tokens * ffn),
         name="mlp",
-    )(attn, h_zero, gain.reshape(1, width), w_o, w_gate, w_up, w_down)
+    )(attn, h_zero, vectors, w_o, w_gate, w_up, w_down)
 
 
 def solution(mesh):
@@ -625,11 +637,13 @@
 
     def local_step(patches, embeds, dest_slot, rope_pos, cu_doc, ln_w, ln_b, w_one, b_one, w_two, b_two, norm_attn, w_q, b_q, w_k, b_k, w_v, b_v, w_o, norm_mlp, w_gate, w_up, w_down):
         heads = w_q.shape[1] // HEAD_DIM
-        h_zero, normed_a = merge_place(group, patches, ln_w, ln_b, w_one, b_one, w_two, b_two, dest_slot, embeds, norm_attn)
+        parts = (ln_w, ln_b, b_one, b_two, norm_attn, b_q, b_k, b_v, norm_mlp)
+        starts = [sum(v.shape[0] for v in parts[:n]) for n in range(len(parts))]
+        vectors = jnp.concatenate([v.astype(jnp.float32) for v in parts]).reshape(1, -1)
         cos_t, sin_t = rope_tables(rope_pos)
-        biases = jnp.concatenate([b.astype(jnp.float32).reshape(heads, 1, HEAD_DIM) for b in (b_q, b_k, b_v)], axis=2)
-        attn_out = mixer(group, heads, cu_doc, normed_a, cos_t, sin_t, biases, w_q, w_k, w_v)
-        return mlp(attn_out, h_zero, norm_mlp, w_o, w_gate, w_up, w_down)
+        h_zero, normed_a = merge_place(group, patches, vectors, w_one, w_two, dest_slot, embeds)
+        attn_out = mixer(group, heads, cu_doc, normed_a, cos_t, sin_t, vectors, tuple(starts[5:8]), w_q, w_k, w_v)
+        return mlp(attn_out, h_zero, vectors, starts[8], w_o, w_gate, w_up, w_down)
 
     in_specs = (row_spec, row_spec, P(('dp', 'sp')), P(None, ('dp', 'sp')), P('dp')) + (P(),) * 18
     return jax.shard_map(local_step, mesh=mesh, in_specs=in_specs, out_specs=row_spec, check_vma=False)

time: 291 us -> 291 us (level)
    reshape x10 -> x1, local copies, waits for them, and re-layouts: 10.4 us -> 0.69 us  [local_step(): jnp.concatenate([v.astype(jnp.float32) for v in parts]).reshape(1, -1)]
    unnamed x10 -> x16, local copies, waits for them, and re-layouts: 0.02 us -> 8.5 us
where the time goes in v3:
time: 291 us; the launch traced here: 290 us
  Pallas kernels  278 us (96%)
  local copies, waits for them, and re-layouts  10.7 us (4%)
    pallas_call x1, Pallas kernels, mixer(): pl.pallas_call(functools.partial(mixer_kernel, group, heads, cu_doc.shape...  142 us
    pallas_call x1, Pallas kernels, merge_place(): pl.pallas_call(functools.partial(merge_place_kernel, group), out_shape=(o...  93.1 us
    pallas_call x1, Pallas kernels, mlp(): pl.pallas_call(functools.partial(mlp_kernel, o_cols, chunk, gain_at), out...  42.9 us
    unnamed x16, local copies, waits for them, and re-layouts  8.5 us

profile of v3, /device:TPU:21, one launch (start us, length us, event | category | flops | bytes accessed | tf_op | source)
XLA Modules:
  0.0 290.2 jit_solution(17646079255068991685)
XLA Ops:
  0.0 0.8 fusion.3
  0.8 0.9 dynamic-update-slice
  1.7 0.9 dynamic-update-slice.1
  2.6 0.9 dynamic-update-slice.2
  3.5 0.9 dynamic-update-slice.3
  4.4 0.9 dynamic-update-slice.4
  5.3 0.9 dynamic-update-slice.5
  6.2 0.9 dynamic-update-slice.6
  7.1 0.9 dynamic-update-slice.7
  8.0 0.7 constant_dynamic-update-slice_fusion
  8.7 0.7 reshape.32.vec_ref
  9.4 0.6 fusion.2
  10.0 0.1 pad_maximum_fusion
  10.2 0.0 copy-start
  10.2 0.0 copy-start.3
  10.2 93.1 %merge_place.1 = (bf16[256,2560]{1,0:T(8,128)(2,1)}, bf16[256,2560]{1,0:T(8,128)(2,1)}) custom-call(bf16[512,1280]{1,0:T(8,128)(2,1)} %patch_ref.1, f32[1,23040]{1,0:T(1,128)} %reshape.32.vec_ref, s32[1,128]{1,0:T(1,128)} %bitcast.7, bf16[256,2560]{1,0:T(8,128)(2,1)} %embeds_ref.1, bf16[5120,5120]{1,0:T(8,128)(2,1)} %w1_ref.1, bf16[5120,2560]{1,0:T(8,128)(2,1)} %w2_ref.1), custom_call_target="tpu_custom_call" | custom-call | flops 10066329600 | bytes 39321600 | tf_op jit(solution)/shard_map/merge_place/pallas_call | solution.py:512
  103.3 0.0 copy-done
  103.4 0.0 copy-done.3
  103.4 0.0 copy-start.2
  103.4 1.3 copy-done.2
  104.7 0.0 copy-start.1
  104.7 142.4 %mixer.1.attn_ref = bf16[20,256,128]{2,1,0:T(8,128)(2,1)S(1)} custom-call(s32[5]{0:T(128)S(1)} %copy-done.3, bf16[256,2560]{1,0:T(8,128)(2,1)S(1)} %copy-done.2, f32[256,128]{1,0:T(8,128)S(1)} %get-tuple-element.15.cos_ref, f32[256,128]{1,0:T(8,128)S(1)} %get-tuple-element.16.sin_ref, f32[1,23040]{1,0:T(1,128)S(1)} %copy-done, bf16[2560,2560]{1,0:T(8,128)(2,1)} %wq_ref.1, ...), custom_call_target="tpu_custom_call" | custom-call | flops 10066329600 | bytes 39321600 | tf_op jit(solution)/shard_map/mixer/pallas_call | solution.py:308
  247.1 0.0 copy-done.1
  247.1 42.9 %mlp.1 = bf16[256,2560]{1,0:T(8,128)(2,1)} custom-call(bf16[20,256,128]{2,1,0:T(8,128)(2,1)S(1)} %mixer.1.attn_ref, bf16[256,2560]{1,0:T(8,128)(2,1)S(1)} %copy-done.1, f32[1,23040]{1,0:T(1,128)S(1)} %copy-done, bf16[2560,2560]{1,0:T(8,128)(2,1)} %wo_ref.1, bf16[2560,6912]{1,0:T(8,128)(2,1)} %wg_ref.1, bf16[2560,6912]{1,0:T(8,128)(2,1)} %wu_ref.1, ...), custom_call_target="tpu_custom_call" | custom-call | flops 30534533120 | bytes 119275520 | tf_op jit(solution)/shard_map/mlp/pallas_call | solution.py:611
  (4 shorter events, 0.0 us)
Async XLA Ops:
  10.2 93.2 %copy-start = (f32[1,23040]{1,0:T(1,128)S(1)}, f32[1,23040]{1,0:T(1,128)}, u32[]{:S(2)}) copy-start(f32[1,23040]{1,0:T(1,128)} %reshape.32.vec_ref) | copy-start | bytes 276484
  10.2 93.2 %copy-start.3 = (s32[5]{0:T(128)S(1)}, s32[5]{0:T(128)}, u32[]{:S(2)}) copy-start(s32[5]{0:T(128)} %cu_ref.1) | copy-start | bytes 64
  103.4 1.3 copy-start.2
  104.7 142.4 %copy-start.1 = (bf16[256,2560]{1,0:T(8,128)(2,1)S(1)}, bf16[256,2560]{1,0:T(8,128)(2,1)}, u32[]{:S(2)}) copy-start(bf16[256,2560]{1,0:T(8,128)(2,1)} %get-tuple-element.8.h_ref) | copy-start | bytes 3932164

commit v4 on v3

--- a/solution.py
+++ b/solution.py
@@ -340,11 +340,12 @@
     other = me + 1 - 2 * core
     ahead = (me + 2 - 4 * core + group) % group
     depth = wbuf.shape[0]
-    part = wbuf.shape[2]
+    part, span = rows.shape[-1], wbuf.shape[2]
     merged_dev, vit = slots_ref.shape[1], patch_ref.shape[1]
     merge_dim, width = w2_ref.shape
-    half_in, half_out = merge_dim // (2 * part), width // (2 * part)
-    count = half_in + half_out
+    half_in, half_out = merge_dim // (2 * span), width // (2 * part)
+    spans = [min(span, width // 2 - at) for at in range(0, width // 2, span)]
+    count = half_in + len(spans)
     after = [0]
     for size in (vit, vit, merge_dim, width, width):
         after.append(after[-1] + size)
@@ -352,14 +353,16 @@
     def vector(n):
         return vec_ref[:, after[n]:after[n + 1]]
 
-    def bias(n, index):
-        return vec_ref[:, pl.ds(pl.multiple_of(after[n] + index * part, HEAD_DIM), part)]
+    def bias(n, at, size):
+        return vec_ref[:, pl.ds(pl.multiple_of(after[n] + at, HEAD_DIM), size)]
 
     def weight_copy(j):
         slot = j % depth
-        w_ref, index = (w1_ref, core * half_in + j) if j < half_in else (w2_ref, core * half_out + j - half_in)
-        cols = pl.ds(pl.multiple_of(index * part, part), part)
-        return pltpu.make_async_copy(w_ref.at[:, cols], wbuf.at[slot], w_sem.at[slot])
+        if j < half_in:
+            w_ref, at, size = w1_ref, core * (merge_dim // 2) + j * span, span
+        else:
+            w_ref, at, size = w2_ref, core * (width // 2) + (j - half_in) * span, spans[j - half_in]
+        return pltpu.make_async_copy(w_ref.at[:, pl.ds(pl.multiple_of(at, HEAD_DIM), size)], wbuf.at[slot, :, pl.ds(0, size)], w_sem.at[slot])
 
     for j in range(depth - 1):
         weight_copy(j).start()
@@ -419,7 +422,7 @@
         weight_copy(j + depth - 1).start()
         weight_copy(j).wait()
         lin = jnp.dot(z[...].reshape(2 * merged_dev, merge_dim), wbuf[j % depth], preferred_element_type=jnp.float32)
-        lin = lin + bias(2, core * half_in + j)
+        lin = lin + bias(2, (core * half_in + j) * span, span)
         inner[core * half_in + j] = (lin * (0.5 * (1.0 + lax.erf(lin * 0.7071067811865476)))).astype(jnp.bfloat16)
         if j > 0:
             inner_copy(j - 1).start()
@@ -427,24 +430,30 @@
     for j in range(half_in):
         arrive(inner.at[(1 - core) * half_in + j], in_recv.at[j])
     for j in range(2 * half_in):
-        wide[:, j * part:(j + 1) * part] = inner[j]
+        wide[:, j * span:(j + 1) * span] = inner[j]
+    made, pending = 0, []
     for j in range(half_in, count):
-        piece = j - half_in
+        size = spans[j - half_in]
         if j + depth - 1 < count:
             weight_copy(j + depth - 1).start()
         weight_copy(j).wait()
-        lin = jnp.dot(wide[...], wbuf[j % depth], preferred_element_type=jnp.float32)
-        rows[core, chip, piece] = (lin + bias(3, core * half_out + piece)).astype(jnp.bfloat16)
-        if piece > 0:
-            ring_copy(0, piece - 1).start()
-            pair_copy(0, piece - 1).start()
+        lin = jnp.dot(wide[...], wbuf[j % depth, :, :size], preferred_element_type=jnp.float32)
+        lin = (lin + bias(3, core * (width // 2) + (j - half_in) * span, size)).astype(jnp.bfloat16)
+        fresh = range(made, made + size // part)
+        for piece in fresh:
+            rows[core, chip, piece] = lin[:, (piece - made) * part:(piece - made + 1) * part]
+        for piece in pending:
+            ring_copy(0, piece).start()
+            pair_copy(0, piece).start()
+        made, pending = made + size // part, fresh
     tokens = embeds_ref.shape[0]
     wanted = me * tokens + lax.broadcasted_iota(jnp.int32, (tokens, 1), 0)
     for k in range(1, group):
         dev = lax.rem(me + k, group)
         arrive(slots.at[dev], slot_recv.at[dev])
-    ring_copy(0, half_out - 1).start()
-    pair_copy(0, half_out - 1).start()
+    for piece in pending:
+        ring_copy(0, piece).start()
+        pair_copy(0, piece).start()
 
     def choose(block):
         return jnp.concatenate([jnp.where(slots[2 * block + n] == wanted, 1.0, 0.0) for n in range(2)], axis=1)
@@ -504,7 +513,8 @@
     tokens = embeds.shape[0]
     part = 2 * HEAD_DIM
     chips = group // 2
-    n_in, n_out = merge_dim // part, width // part
+    span = 2 * part
+    n_in, n_out = merge_dim // span, width // part
     vmem = pl.BlockSpec(memory_space=pltpu.VMEM)
     hbm = pl.BlockSpec(memory_space=pl.ANY)
     out = jax.ShapeDtypeStruct((tokens, width), jnp.bfloat16)
@@ -517,8 +527,8 @@
         scratch_shapes=[
             pltpu.VMEM((2, merged_dev, merge_dim), jnp.bfloat16),
             pltpu.VMEM((patches.shape[1] // HEAD_DIM, patches.shape[0], HEAD_DIM), jnp.float32),
-            pltpu.VMEM((3, merge_dim, part), jnp.bfloat16),
-            pltpu.VMEM((n_in, 2 * merged_dev, part), jnp.bfloat16),
+            pltpu.VMEM((3, merge_dim, span), jnp.bfloat16),
+            pltpu.VMEM((n_in, 2 * merged_dev, span), jnp.bfloat16),
             pltpu.VMEM((2 * merged_dev, merge_dim), jnp.bfloat16),
             pltpu.VMEM((2, chips, n_out // 2, 2 * merged_dev, part), jnp.bfloat16),
             pltpu.VMEM((group, 1, merged_dev), jnp.int32),
@@ -639,7 +649,8 @@
         heads = w_q.shape[1] // HEAD_DIM
         parts = (ln_w, ln_b, b_one, b_two, norm_attn, b_q, b_k, b_v, norm_mlp)
         starts = [sum(v.shape[0] for v in parts[:n]) for n in range(len(parts))]
-        vectors = jnp.concatenate([v.astype(jnp.float32) for v in parts]).reshape(1, -1)
+        length = starts[-1] + parts[-1].shape[0]
+        vectors = sum(jnp.pad(v.astype(jnp.float32), (at, length - at - v.shape[0])) for at, v in zip(starts, parts)).reshape(1, length)
         cos_t, sin_t = rope_tables(rope_pos)
         h_zero, normed_a = merge_place(group, patches, vectors, w_one, w_two, dest_slot, embeds)
         attn_out = mixer(group, heads, cu_doc, normed_a, cos_t, sin_t, vectors, tuple(starts[5:8]), w_q, w_k, w_v)

time: 291 us -> 277 us (0.952)
  local copies, waits for them, and re-layouts: 10.7 us -> 2.83 us
  Pallas kernels: 278 us -> 272 us
    unnamed x16 -> x8, local copies, waits for them, and re-layouts: 8.5 us -> 1.33 us
    pallas_call x1, Pallas kernels: 93.1 us -> 86.8 us  [merge_place(): pl.pallas_call(functools.partial(merge_place_kernel, group), out_shape=(o...]
where the time goes in v4:
time: 277 us
  Pallas kernels  272 us (98%)
  local copies, waits for them, and re-layouts  2.83 us (1%)
    pallas_call x1, Pallas kernels, mixer(): pl.pallas_call(functools.partial(mixer_kernel, group, heads, cu_doc.shape...  142 us
    pallas_call x1, Pallas kernels, merge_place(): pl.pallas_call(functools.partial(merge_place_kernel, group), out_shape=(o...  86.8 us
    pallas_call x1, Pallas kernels, mlp(): pl.pallas_call(functools.partial(mlp_kernel, o_cols, chunk, gain_at), out...  42.9 us

profile of v4, /device:TPU:21, one launch (start us, length us, event | category | flops | bytes accessed | tf_op | source)
XLA Modules:
  0.0 276.7 jit_solution(1405771436520770587)
XLA Ops:
  0.0 0.8 fusion.3
  0.8 0.8 convert_add_fusion
  1.7 0.7 reshape.26.vec_ref
  2.4 0.6 fusion.2
  3.0 0.1 pad_maximum_fusion
  3.1 0.0 copy-start
  3.2 0.0 copy-start.3
  3.2 86.8 %merge_place.1 = (bf16[256,2560]{1,0:T(8,128)(2,1)}, bf16[256,2560]{1,0:T(8,128)(2,1)}) custom-call(bf16[512,1280]{1,0:T(8,128)(2,1)} %patch_ref.1, f32[1,23040]{1,0:T(1,128)} %reshape.26.vec_ref, s32[1,128]{1,0:T(1,128)} %bitcast.7, bf16[256,2560]{1,0:T(8,128)(2,1)} %embeds_ref.1, bf16[5120,5120]{1,0:T(8,128)(2,1)} %w1_ref.1, bf16[5120,2560]{1,0:T(8,128)(2,1)} %w2_ref.1), custom_call_target="tpu_custom_call" | custom-call | flops 10066329600 | bytes 39321600 | tf_op jit(solution)/shard_map/merge_place/pallas_call | solution.py:522
  90.0 0.0 copy-done
  90.0 0.0 copy-done.3
  90.0 0.0 copy-start.2
  90.0 1.3 copy-done.2
  91.3 0.0 copy-start.1
  91.3 142.2 %mixer.1.attn_ref = bf16[20,256,128]{2,1,0:T(8,128)(2,1)S(1)} custom-call(s32[5]{0:T(128)S(1)} %copy-done.3, bf16[256,2560]{1,0:T(8,128)(2,1)S(1)} %copy-done.2, f32[256,128]{1,0:T(8,128)S(1)} %get-tuple-element.15.cos_ref, f32[256,128]{1,0:T(8,128)S(1)} %get-tuple-element.16.sin_ref, f32[1,23040]{1,0:T(1,128)S(1)} %copy-done, bf16[2560,2560]{1,0:T(8,128)(2,1)} %wq_ref.1, ...), custom_call_target="tpu_custom_call" | custom-call | flops 10066329600 | bytes 39321600 | tf_op jit(solution)/shard_map/mixer/pallas_call | solution.py:308
  233.6 0.0 copy-done.1
  233.6 42.9 %mlp.1 = bf16[256,2560]{1,0:T(8,128)(2,1)} custom-call(bf16[20,256,128]{2,1,0:T(8,128)(2,1)S(1)} %mixer.1.attn_ref, bf16[256,2560]{1,0:T(8,128)(2,1)S(1)} %copy-done.1, f32[1,23040]{1,0:T(1,128)S(1)} %copy-done, bf16[2560,2560]{1,0:T(8,128)(2,1)} %wo_ref.1, bf16[2560,6912]{1,0:T(8,128)(2,1)} %wg_ref.1, bf16[2560,6912]{1,0:T(8,128)(2,1)} %wu_ref.1, ...), custom_call_target="tpu_custom_call" | custom-call | flops 30534533120 | bytes 119275520 | tf_op jit(solution)/shard_map/mlp/pallas_call | solution.py:621
  (3 shorter events, 0.0 us)
Async XLA Ops:
  3.1 86.9 %copy-start = (f32[1,23040]{1,0:T(1,128)S(1)}, f32[1,23040]{1,0:T(1,128)}, u32[]{:S(2)}) copy-start(f32[1,23040]{1,0:T(1,128)} %reshape.26.vec_ref) | copy-start | bytes 276484
  3.2 86.9 %copy-start.3 = (s32[5]{0:T(128)S(1)}, s32[5]{0:T(128)}, u32[]{:S(2)}) copy-start(s32[5]{0:T(128)} %cu_ref.1) | copy-start | bytes 64
  90.0 1.3 copy-start.2
  91.3 142.2 %copy-start.1 = (bf16[256,2560]{1,0:T(8,128)(2,1)S(1)}, bf16[256,2560]{1,0:T(8,128)(2,1)}, u32[]{:S(2)}) copy-start(bf16[256,2560]{1,0:T(8,128)(2,1)} %get-tuple-element.8.h_ref) | copy-start | bytes 3932164
